TPU v7x, 32 devices: a 4x4x1 block of a 4x4x8 slice. The times are simulated.
32 devices in a mesh: sys: 1 (over z), aux: 4 (over y), orb: 8 (over x, core).
Axes of the slice: x: 4, y: 4, z: 1, core: 2. Of those that a mesh axis runs over, the one named last changes fastest.
The devices are a block of a 4x4x8 slice.
Arguments:
- aux_ints: float32 [1344, 384, 384], P(('sys', 'aux'), 'orb')
- metric: float32 [1344, 1344], P(('sys', 'aux'))
- orbitals: float32 [4, 384, 80], P('sys')
Outputs:
- output: float32 [4, 384, 384], P('sys', 'orb', 'aux')
All inputs are finite; a program needn't handle non-finite values.
Results may differ from a plain program's by a relative error of at most 0.001.
Values are sent between devices in bfloat16 or wider.
A program may use at most 768 MiB of HBM per device.

v0:
```python
import jax
import jax.numpy as jnp
from jax import lax
from jax.experimental import pallas as pl
from jax.experimental.pallas import tpu as pltpu
from jax.sharding import PartitionSpec as P

PRECISE = lax.Precision.HIGHEST
F32 = jnp.float32
BF16 = jnp.bfloat16
MESH = pl.DeviceIdType.MESH
LANES = 128
WIDE = 256
SUB = 8
Q_TILE = 112


def round_up(n, to):
    return (n + to - 1) // to * to


def parts3(x):
    hi = x.astype(BF16)
    rest = x - hi.astype(F32)
    mid = rest.astype(BF16)
    return hi, mid, (rest - mid.astype(F32)).astype(BF16)


def split3(x):
    hi = lax.reduce_precision(x, 8, 7)
    mid = lax.reduce_precision(x - hi, 8, 7)
    return hi.astype(BF16), mid.astype(BF16), (x - hi - mid).astype(BF16)


def fit_exchange(ints, c_cat, c_rows, pick, weights, n_aux, n_orb, n_i):
    n_q, n_g, sub, n_l = ints.shape
    n_c = n_g // 2
    n_m = n_g * sub
    depth, n_p = weights.shape
    n_di = c_cat.shape[1]
    n_v = n_di // LANES
    n_d = n_aux
    pad_q = (n_q // Q_TILE) * LANES
    n_t = n_q // Q_TILE
    n_rows = n_i * 2 * sub
    share = n_rows // n_orb
    half_rows = n_rows // 2
    half_orb = n_orb // 2
    own_at = (n_aux - 1) * pad_q
    n_g_rows = pick.shape[0]

    def kernel(b_ref, c_ref, crow_ref, pick_ref, w_hbm, t_ref, mine_ref, j_ref,
               b_buf, w_ref, t_buf, temp, acc, send, part, got, fit, out, g_send, g_got, f_send, f_got, w_vec, w_smem,
               y_send, y_recv, x_send, x_recv, gx_send, gx_recv, gy_send, gy_recv, loc, keep):
        j, k = lax.axis_index('aux'), lax.axis_index('orb')
        load_w = pltpu.make_async_copy(w_hbm, w_ref, loc.at[1])

        def load_b(c):
            return pltpu.make_async_copy(b_ref.at[:, pl.ds(2 * c, 2)], b_buf, loc.at[0])

        load_b(0).start()
        load_w.start()
        barrier = pltpu.get_barrier_semaphore()
        for r in range(1, n_aux):
            pl.semaphore_signal(barrier, inc=1, device_id={'aux': lax.rem(j + r, n_aux)}, device_id_type=MESH)
        for r in range(1, n_orb):
            pl.semaphore_signal(barrier, inc=1, device_id={'orb': lax.rem(k + r, n_orb)}, device_id_type=MESH)

        def y_copy(c, r):
            to = lax.rem(j + n_aux - r, n_aux)
            return pltpu.make_async_remote_copy(
                src_ref=send.at[c % 2, to], dst_ref=got.at[c, r - 1], send_sem=y_send.at[c, r - 1],
                recv_sem=y_recv.at[c, r - 1], device_id={'aux': to}, device_id_type=MESH)

        def x_copy(c, r):
            to = lax.rem(k + r, n_orb)
            return pltpu.make_async_remote_copy(
                src_ref=out.at[c % 2, to], dst_ref=t_ref.at[k, c], send_sem=x_send.at[c, r - 1],
                recv_sem=x_recv.at[c, r - 1], device_id={'orb': to}, device_id_type=MESH)

        def gx_copy(r):
            return pltpu.make_async_remote_copy(
                src_ref=g_send, dst_ref=g_got.at[r - 1], send_sem=gx_send.at[r - 1], recv_sem=gx_recv.at[r - 1],
                device_id={'orb': lax.rem(k + r, n_orb)}, device_id_type=MESH)

        def gy_copy(r):
            return pltpu.make_async_remote_copy(
                src_ref=f_send, dst_ref=f_got.at[r - 1], send_sem=gy_send.at[r - 1], recv_sem=gy_recv.at[r - 1],
                device_id={'aux': lax.rem(j + r, n_aux)}, device_id_type=MESH)

        def keep_copies(c):
            return (pltpu.make_async_copy(fit.at[lax.rem(k, half_orb)], mine_ref.at[c], keep.at[0]),
                    pltpu.make_async_copy(out.at[c % 2, k], t_ref.at[k, c], keep.at[1]))

        acc[...] = jnp.zeros_like(acc)
        t_buf[:, Q_TILE * sub:, :] = jnp.zeros((n_v, (LANES - Q_TILE) * sub, LANES), F32)

        def transform(c):
            load_b(c).wait()
            if c >= 2:
                for r in range(1, n_aux):
                    y_copy(c - 2, r).wait_send()

            @pl.loop(0, n_t)
            def _(t):
                lanes = pl.ds(pl.multiple_of(t * LANES, LANES), LANES)

                @pl.loop(0, 2)
                def _(h):
                    q_rows = pl.ds(pl.multiple_of(t * Q_TILE, Q_TILE), Q_TILE)
                    hi, mid, low = parts3(b_buf[q_rows, h, :, :].reshape(Q_TILE * sub, n_l))
                    left = jnp.concatenate([hi, hi, hi, mid, mid, low], axis=1)
                    res = jnp.dot(left, c_ref[...], preferred_element_type=F32)
                    for v in range(n_v):
                        t_buf[v, 0:Q_TILE * sub, :] = res[:, v * LANES:(v + 1) * LANES]
                    for v in range(n_v):
                        part_di = slice(v * LANES, (v + 1) * LANES)
                        c_row = crow_ref[2 * c + h, :, part_di]
                        live = min(LANES, n_d * n_i - v * LANES)
                        total = acc[t, :, part_di]
                        for m in range(sub):
                            row = t_buf[v, pl.ds(m, LANES, stride=sub), :]
                            total += row * c_row[m:m + 1, :]
                            temp[h, pl.ds(v * LANES * sub + m, live, stride=sub), :] = row.T[:live, :]
                        acc[t, :, part_di] = total

                for d in range(n_d):
                    rows = pl.ds(d * n_i * sub, n_i * sub)
                    both = jnp.concatenate([temp[h, rows, :].reshape(n_i, sub, LANES) for h in range(2)], axis=1)
                    send[c % 2, d, :, lanes] = both.reshape(n_rows, LANES).astype(BF16)
                rows = pl.ds(pl.multiple_of(j * (n_i * sub), n_i * sub), n_i * sub)
                both = jnp.concatenate([temp[h, rows, :].reshape(n_i, sub, LANES) for h in range(2)], axis=1)
                for p, piece in enumerate(parts3(both.reshape(n_rows, LANES))):
                    part[c % 2, :, pl.ds(pl.multiple_of(p * pad_q + t * LANES, LANES), LANES)] = piece

            if c + 1 < n_c:
                load_b(c + 1).start()

        def fit_chunk(c):
            for r in range(1, n_aux):
                y_copy(c, r).wait_recv()
            if c > 0:
                for copy in keep_copies(c - 1):
                    copy.wait()
            if c >= 2:
                for r in range(1, n_orb):
                    x_copy(c - 2, r).wait_send()

            def tile(h, start, width):
                rows = pl.ds(pl.multiple_of(h * half_rows, half_rows), half_rows)
                cols = pl.ds(start, width)
                hi, mid, low = [part[c % 2, rows, p * pad_q:(p + 1) * pad_q] for p in range(3)]
                left = jnp.concatenate([got[c, r, rows, :] for r in range(n_aux - 1)] + [hi, hi, hi, mid, mid, low], axis=1)
                res = jnp.dot(left, w_ref[:, cols], preferred_element_type=F32).reshape(half_orb, share, width)
                out[c % 2, pl.ds(h * half_orb, half_orb), :, cols] = res.astype(BF16)

                @pl.when(h == k // half_orb)
                def _():
                    fit[:, :, cols] = res

            @pl.loop(0, 2)
            def _(h):
                @pl.loop(0, n_p // WIDE)
                def _(n):
                    tile(h, pl.multiple_of(n * WIDE, WIDE), WIDE)
                if n_p % WIDE:
                    tile(h, n_p // WIDE * WIDE, n_p % WIDE)

            for r in range(1, n_orb):
                x_copy(c, r).start()
            for copy in keep_copies(c):
                copy.start()

        def send_y(c):
            for r in range(1, n_aux):
                y_copy(c, r).start()

        nt = (((1,), (1,)), ((), ()))
        transform(0)
        pl.semaphore_wait(barrier, n_aux + n_orb - 2)
        send_y(0)
        transform(1)
        send_y(1)
        load_w.wait()
        fit_chunk(0)
        transform(2)
        send_y(2)
        load_b(0).start()
        g_send[...] = lax.dot_general(pick_ref[...], acc[...].reshape(n_t * LANES, n_di), nt, precision=PRECISE, preferred_element_type=F32)
        for r in range(1, n_orb):
            gx_copy(r).start()
        fit_chunk(1)
        for r in range(1, n_orb):
            gx_copy(r).wait()
        gamma = g_send[...]
        for r in range(1, n_orb):
            gamma += g_got[r - 1]
        hi, mid, low = parts3(gamma)
        left = jnp.concatenate([hi, hi, hi, mid, mid, low], axis=1)
        f_send[...] = jnp.dot(left, w_ref[own_at:, :], preferred_element_type=F32)
        for r in range(1, n_aux):
            gy_copy(r).start()
        for r in range(1, n_aux):
            gy_copy(r).wait()
        gamma_fit = f_send[...]
        for r in range(1, n_aux):
            gamma_fit += f_got[r - 1]
        hi, mid, low = parts3(gamma_fit)
        m_hi, m_mid, m_low = [w_ref[own_at + p * pad_q:own_at + (p + 1) * pad_q, :] for p in range(3)]
        by_hi = lax.dot_general(jnp.concatenate([hi, mid, low], axis=0), m_hi, nt, preferred_element_type=F32)
        by_mid = lax.dot_general(jnp.concatenate([hi, mid], axis=0), m_mid, nt, preferred_element_type=F32)
        by_low = lax.dot_general(hi, m_low, nt, preferred_element_type=F32)
        n = n_g_rows
        small = by_low + by_mid[n:] + by_hi[2 * n:]
        w_vec[...] = by_hi[:n] + ((by_hi[n:2 * n] + by_mid[:n]) + small)
        to_smem = pltpu.make_async_copy(w_vec, w_smem, loc.at[2])
        to_smem.start()
        to_smem.wait()
        for c in range(n_c):
            load_b(c).wait()
            for h in range(2):
                total = [jnp.zeros((sub, n_l), F32) for _ in range(n_d)]
                for t in range(n_t):
                    def some(s, total):
                        total = list(total)
                        for u in range(8):
                            q = s * 8 + u
                            block = b_buf[t * Q_TILE + q, h]
                            for d in range(n_d):
                                total[d] = total[d] + block * w_smem[d, t * LANES + q]
                        return tuple(total)
                    total = lax.fori_loop(0, Q_TILE // 8, some, tuple(total))
                for d in range(n_d):
                    j_ref[d, (2 * c + h) * sub:(2 * c + h + 1) * sub, :] = total[d]
            if c + 1 < n_c:
                load_b(c + 1).start()
        fit_chunk(2)

        for copy in keep_copies(n_c - 1):
            copy.wait()
        for c in range(n_c):
            for r in range(1, n_aux):
                if c >= n_c - 2:
                    y_copy(c, r).wait_send()
            for r in range(1, n_orb):
                if c >= n_c - 2:
                    x_copy(c, r).wait_send()
                x_copy(c, r).wait_recv()

    any_spec = pl.BlockSpec(memory_space=pl.ANY)
    vmem = pl.BlockSpec(memory_space=pltpu.VMEM)
    dma = pltpu.SemaphoreType.DMA
    return pl.pallas_call(
        kernel,
        out_shape=(jax.ShapeDtypeStruct((n_orb, n_c, share, n_p), BF16), jax.ShapeDtypeStruct((n_c, share, n_p), F32),
                   jax.ShapeDtypeStruct((n_d, n_m, n_l), F32)),
        in_specs=[any_spec, vmem, vmem, vmem, any_spec],
        out_specs=(any_spec, any_spec, vmem),
        scratch_shapes=[
            pltpu.VMEM((n_q, 2, sub, n_l), F32),
            pltpu.VMEM((depth, n_p), BF16),
            pltpu.VMEM((n_v, LANES * sub, LANES), F32),
            pltpu.VMEM((2, n_d * n_i * sub, LANES), F32),
            pltpu.VMEM((n_t, LANES, n_di), F32),
            pltpu.VMEM((2, n_d, n_rows, pad_q), BF16),
            pltpu.VMEM((2, n_rows, 3 * pad_q), BF16),
            pltpu.VMEM((n_c, n_aux - 1, n_rows, pad_q), BF16),
            pltpu.VMEM((half_orb, share, n_p), F32),
            pltpu.VMEM((2, n_orb, share, n_p), BF16),
            pltpu.VMEM((n_g_rows, pad_q), F32), pltpu.VMEM((n_orb - 1, n_g_rows, pad_q), F32),
            pltpu.VMEM((n_g_rows, n_p), F32), pltpu.VMEM((n_aux - 1, n_g_rows, n_p), F32),
            pltpu.VMEM((n_g_rows, pad_q), F32), pltpu.SMEM((n_g_rows, pad_q), F32),
            dma((n_c, n_aux - 1)), dma((n_c, n_aux - 1)), dma((n_c, n_orb - 1)), dma((n_c, n_orb - 1)),
            dma((n_orb - 1,)), dma((n_orb - 1,)), dma((n_aux - 1,)), dma((n_aux - 1,)),
            dma((3,)), dma((2,)),
        ],
        compiler_params=pltpu.CompilerParams(collective_id=0, has_side_effects=True, vmem_limit_bytes=67043328),
    )(ints, c_cat, c_rows, pick, weights)


def gram(t, mine):
    n_k, n_c, n_i, n_r, n_p = t.shape
    n_m, n_n = n_c * n_r, n_k * n_c * n_r

    def kernel(t_ref, mine_ref, o_ref, s_ref):
        all_t = t_ref[...].reshape(n_n, n_p)
        own = mine_ref[...].reshape(n_m, n_p)
        rest = own - own.astype(BF16).astype(F32)
        mid = rest.astype(BF16)
        low = (rest - mid.astype(F32)).astype(BF16)
        left = jnp.concatenate([all_t, mid, low], axis=0)
        nt = (((1,), (1,)), ((), ()))
        res = lax.dot_general(left, all_t, nt, preferred_element_type=F32)
        sq = lax.dot_general(mid, mid, nt, preferred_element_type=F32)

        @pl.when(pl.program_id(0) == 0)
        def _():
            o_ref[...] = res
            s_ref[...] = sq

        @pl.when(pl.program_id(0) > 0)
        def _():
            o_ref[...] += res
            s_ref[...] += sq

    return pl.pallas_call(
        kernel,
        grid=(n_i,),
        out_shape=(jax.ShapeDtypeStruct((n_n + 2 * n_m, n_n), F32), jax.ShapeDtypeStruct((n_m, n_m), F32)),
        in_specs=[pl.BlockSpec((n_k, n_c, 1, n_r, n_p), lambda i: (0, 0, i, 0, 0)),
                  pl.BlockSpec((n_c, 1, n_r, n_p), lambda i: (0, i, 0, 0))],
        out_specs=(pl.BlockSpec((n_n + 2 * n_m, n_n), lambda i: (0, 0)), pl.BlockSpec((n_m, n_m), lambda i: (0, 0))),
        compiler_params=pltpu.CompilerParams(vmem_limit_bytes=32 * 2**20),
    )(t, mine)


def solution(mesh):
    n_aux, n_orb = mesh.shape['aux'], mesh.shape['orb']

    def local_fock(ints, metric, orbitals):
        n_q, n_m, n_l = ints.shape
        n_d, _, n_i = orbitals.shape
        n_n, n_p = n_orb * n_m, n_aux * n_q
        n_c = n_m // (2 * SUB)
        pad_p = round_up(n_p, LANES)
        n_t = n_q // Q_TILE
        pad_q = n_t * LANES
        pad_di = round_up(n_d * n_i, LANES)
        j, k = lax.axis_index('aux'), lax.axis_index('orb')

        metric_pad = jnp.pad(metric.reshape(n_t, Q_TILE, n_p), ((0, 0), (0, LANES - Q_TILE), (0, pad_p - n_p))).reshape(pad_q, pad_p)
        m_hi, m_mid, m_low = split3(metric_pad)
        met = lax.all_gather(m_hi, 'aux', axis=0)
        met = jnp.concatenate([met, met], axis=0)
        met = lax.dynamic_slice_in_dim(met, j + 1, n_aux - 1, axis=0).reshape((n_aux - 1) * pad_q, pad_p)
        fit_w = jnp.concatenate([met, m_hi, m_mid, m_low, m_hi, m_mid, m_hi], axis=0)

        c_all = jnp.pad(orbitals.transpose(1, 0, 2).reshape(n_l, n_d * n_i), ((0, 0), (0, pad_di - n_d * n_i)))
        c_hi, c_mid, c_low = split3(c_all)
        c_cat = jnp.concatenate([c_hi, c_mid, c_low, c_hi, c_mid, c_hi], axis=0)
        c_rows = lax.dynamic_slice_in_dim(c_all, k * n_m, n_m, axis=0)
        lane = jnp.arange(pad_di)[None, :] // n_i
        pick = (lane == jnp.arange(2 * SUB)[:, None]).astype(F32)
        all_t, mine, coul = fit_exchange(ints.reshape(n_q, n_m // SUB, SUB, n_l), c_cat, c_rows.reshape(n_m // SUB, SUB, pad_di), pick, fit_w, n_aux, n_orb, n_i)
        coul = lax.psum_scatter(coul, 'aux', scatter_dimension=2, tiled=True)
        all_t = all_t.reshape(n_orb, n_c, n_i // n_orb, 2 * SUB, pad_p)
        mine = mine.reshape(n_c, n_i // n_orb, 2 * SUB, pad_p)
        exch, own_sq = gram(all_t, mine)
        cross = exch[n_n:n_n + n_m] + exch[n_n + n_m:]
        own_sq = lax.dynamic_update_slice_in_dim(jnp.zeros((n_m, n_n), F32), 0.5 * own_sq, k * n_m, axis=1)
        cross = lax.dynamic_update_slice_in_dim(jnp.zeros((n_n, n_n), F32), cross + own_sq, k * n_m, axis=0)
        exch = exch[:n_n] + cross + cross.T
        exch = lax.psum_scatter(exch, 'orb', scatter_dimension=0, tiled=True)
        exch = lax.all_to_all(exch.reshape(n_m, n_aux, n_n // n_aux), 'aux', 1, 0)
        return 2.0 * coul - exch.reshape(n_d, n_m, n_n // n_aux)

    return jax.shard_map(local_fock, mesh=mesh, in_specs=(P(('sys', 'aux'), 'orb', None), P(('sys', 'aux'), None), P('sys', None, None)), out_specs=P('sys', 'orb', 'aux'), check_vma=False)
```

profile of v0, /device:TPU:97, one launch (start us, length us, event | category | flops | bytes accessed | tf_op | source)
XLA Modules:
  0.0 377.5 jit_solution(13059413566223721420)
XLA Ops:
  6.6 3.5 fusion.9
  10.0 0.1 all-gather.2.cloned.1.call-update
  10.1 0.1 reduce-scatter.5.cloned.1.call-start
  10.2 0.2 copy.10
  10.4 0.6 fusion.4.crow_ref
  11.1 0.1 constant_dynamic-update-slice_fusion.3
  11.2 0.1 fusion.3
  11.4 0.1 constant_dynamic-update-slice_fusion.2
  11.4 0.1 constant_dynamic-update-slice_fusion.1
  11.5 0.1 constant_dynamic-update-slice_fusion.c_ref
  11.6 0.6 fusion.5.pick_ref
  12.2 0.6 copy-done.4
  12.8 0.4 copy-done.3
  13.2 0.5 fusion.1
  13.7 46.9 %all-gather.2.cloned.1.call-done = bf16[4,384,1408]{2,1,0:T(8,128)(2,1)} async-done(((bf16[1,384,1408]{2,1,0:T(8,128)(2,1)}), bf16[4,384,1408]{2,1,0:T(8,128)(2,1)}) %all-gather.2.cloned.1.call-update) | async-done | bytes 4325392 | tf_op jit(solution)/shard_map/all_gather | solution.py:333
  60.6 3.2 fusion
  63.8 0.2 constant_dynamic-update-slice_fusion.11
  64.1 0.1 constant_dynamic-update-slice_fusion.10
  64.2 0.1 constant_dynamic-update-slice_fusion.9
  64.4 0.1 constant_dynamic-update-slice_fusion.8
  64.5 0.1 constant_dynamic-update-slice_fusion.7
  64.7 0.1 constant_dynamic-update-slice_fusion.6
  64.9 0.1 constant_dynamic-update-slice_fusion.5.w_hbm
  65.0 3.6 copy-done.2
  68.6 234.4 %shard_map.37 = (bf16[8,3,160,1408]{3,2,1,0:T(8,128)(2,1)}, f32[3,160,1408]{2,1,0:T(8,128)}, f32[4,48,384]{2,1,0:T(8,128)}) custom-call(f32[336,6,8,384]{3,2,1,0:T(8,128)} %bitcast.30, bf16[2304,384]{1,0:T(8,128)(2,1)} %copy-done.4, f32[6,8,384]{2,1,0:T(8,128)} %fusion.4.crow_ref, f32[16,384]{1,0:T(8,128)} %fusion.5.pick_ref, bf16[3456,1408]{1,0:T(8,128)(2,1)} %copy-done.2), custom_call_target="tpu_custom_call" | custom-call | tf_op jit(solution)/shard_map/pallas_call | solution.py:253
  303.1 4.1 %copy-done = bf16[8,3,160,1408]{3,2,1,0:T(8,128)(2,1)S(1)} copy-done((bf16[8,3,160,1408]{3,2,1,0:T(8,128)(2,1)S(1)}, bf16[8,3,160,1408]{3,2,1,0:T(8,128)(2,1)}, u32[]{:S(2)}) %copy-start) | copy-done | bytes 10813464
  307.1 1.8 copy-done.1
  308.9 11.5 %shard_map.38 = (f32[480,384]{1,0:T(8,128)S(1)}, f32[48,48]{1,0:T(8,128)S(1)}) custom-call(bf16[8,3,10,16,1408]{4,3,2,1,0:T(8,128)(2,1)S(1)} %bitcast.28, f32[3,10,16,1408]{3,2,1,0:T(8,128)S(1)} %bitcast.29), custom_call_target="tpu_custom_call" | custom-call | tf_op jit(solution)/shard_map/pallas_call | solution.py:306
  320.4 0.0 copy-start.6
  320.5 0.1 multiply_add_fusion
  320.5 0.5 add.48
  321.1 0.1 copy.11
  321.3 1.8 dynamic_update_slice.10
  323.1 0.9 bitcast_add_fusion
  324.0 0.1 reduce-scatter.5.cloned.1.call-update
  324.1 0.1 reduce-scatter.7.cloned.1.call-start
  324.2 0.3 copy.13
  324.5 1.1 reshape.71
  325.6 0.1 reduce-scatter.7.cloned.1.call-update
  325.7 23.2 %reduce-scatter.5.cloned.1.call-done = f32[48,384]{1,0:T(8,128)} async-done(((f32[384,384]{1,0:T(8,128)}), f32[48,384]{1,0:T(8,128)}) %reduce-scatter.5.cloned.1.call-update) | async-done | bytes 73744 | tf_op jit(solution)/shard_map/reduce_scatter | solution.py:353
  348.8 1.0 broadcast_in_dim_reshape.3
  349.8 0.6 copy.12
  350.5 4.4 %all-to-all-start = ((f32[1,48,4,96]{3,1,0,2:T(8,128)}), f32[1,48,4,96]{3,1,0,2:T(8,128)S(1)}, u32[]{:S(2)}, u32[]{:S(2)}) async-start(f32[1,48,4,96]{3,1,0,2:T(8,128)} %copy.12), calls=%async_computation.1 | async-start | bytes 196608 | tf_op jit(solution)/shard_map/all_to_all | solution.py:354
  354.9 14.3 %reduce-scatter.7.cloned.1.call-done = f32[96,192]{1,0:T(8,128)} async-done(((f32[384,192]{1,0:T(8,128)}), f32[96,192]{1,0:T(8,128)}) %reduce-scatter.7.cloned.1.call-update) | async-done | bytes 73744
  369.1 1.0 reshape.72
  370.2 0.1 copy.14
  370.3 0.0 all-to-all-done
  370.3 0.7 bitcast_subtract_fusion
  (15 shorter events, 0.2 us)
Async XLA Ops:
  6.5 54.0 %all-gather.2.cloned.1.call-start = ((), (), s32[]{:S(2)}) async-start(), calls=%async_computation.3 | async-start | bytes 5406720 | tf_op jit(solution)/shard_map/all_gather | solution.py:333
  6.6 3.6 copy-start.5
  10.1 338.7 %reduce-scatter.5.cloned.1.call-start = ((), (), s32[]{:S(2)}) async-start(), calls=%async_computation.4 | async-start | bytes 663552 | tf_op jit(solution)/shard_map/reduce_scatter | solution.py:353
  11.1 2.1 copy-start.3
  11.6 1.2 copy-start.4
  65.0 3.6 copy-start.2
  303.1 4.1 %copy-start = (bf16[8,3,160,1408]{3,2,1,0:T(8,128)(2,1)S(1)}, bf16[8,3,160,1408]{3,2,1,0:T(8,128)(2,1)}, u32[]{:S(2)}) copy-start(bf16[8,3,160,1408]{3,2,1,0:T(8,128)(2,1)} %get-tuple-element.11) | copy-start | bytes 32440324
  307.1 1.8 copy-start.1
  320.4 3.7 copy-start.6
  324.1 45.1 %reduce-scatter.7.cloned.1.call-start = ((), (), s32[]{:S(2)}) async-start(), calls=%async_computation.5 | async-start | bytes 491520
  350.5 19.8 %all-to-all-start = ((f32[1,48,4,96]{3,1,0,2:T(8,128)}), f32[1,48,4,96]{3,1,0,2:T(8,128)S(1)}, u32[]{:S(2)}, u32[]{:S(2)}) async-start(f32[1,48,4,96]{3,1,0,2:T(8,128)} %copy.12), calls=%async_computation.1 | async-start | bytes 196608 | tf_op jit(solution)/shard_map/all_to_all | solution.py:354
Sparse Core Ops, SparseCore 0:
  10.2 50.3 all-gather.1
  324.2 24.5 reduce-scatter.4
  351.1 17.9 reduce-scatter.6
where the time goes:
time: 379 us; the launch traced here: 378 us
  Pallas kernels  246 us (65%)
  waiting for transfers between devices  84.5 us (22%)
  local copies, waits for them, and re-layouts  19.2 us (5%)
  between operations  13.4 us (4%)
  other arithmetic  9.95 us (3%)
  starting transfers between devices  4.52 us (1%)
    pallas_call x1, Pallas kernels, fit_exchange(): pl.pallas_call(kernel, out_shape=(jax.ShapeDtypeStruct((n_orb, n_c, share...  234 us
    all_gather x1, waiting for transfers between devices, local_fock(): met = lax.all_gather(m_hi, 'aux', axis=0)  46.9 us
    reduce_scatter x1, waiting for transfers between devices, local_fock(): exch = lax.psum_scatter(exch, 'orb', scatter_dimension=0, tiled=True)  23.2 us
    unnamed x4, waiting for transfers between devices  14.4 us
    unnamed x24, local copies, waits for them, and re-layouts  14 us
    pallas_call x1, Pallas kernels, gram(): pl.pallas_call(kernel, grid=(n_i,), out_shape=(jax.ShapeDtypeStruct((n_n...  11.5 us
  transfers between devices with their start and end apart: 4, of which 3 were waited for; matrix products, arithmetic and copies ran while one was open for 2% of the time, Pallas kernels for 0%

commit v1 on v0

v1 whole, which is shorter than its diff:
```python
import jax
import jax.numpy as jnp
from jax import lax
from jax.experimental import pallas as pl
from jax.experimental.pallas import tpu as pltpu
from jax.sharding import PartitionSpec as P

PRECISE = lax.Precision.HIGHEST
F32 = jnp.float32
BF16 = jnp.bfloat16
MESH = pl.DeviceIdType.MESH
LANES = 128
WIDE = 256
SUB = 8
Q_TILE = 112


def round_up(n, to):
    return (n + to - 1) // to * to


def parts3(x):
    hi = x.astype(BF16)
    rest = x - hi.astype(F32)
    mid = rest.astype(BF16)
    return hi, mid, (rest - mid.astype(F32)).astype(BF16)


def split3(x):
    hi = lax.reduce_precision(x, 8, 7)
    mid = lax.reduce_precision(x - hi, 8, 7)
    return hi.astype(BF16), mid.astype(BF16), (x - hi - mid).astype(BF16)


def fit_exchange(ints, c_cat, c_rows, pick, weights, n_aux, n_orb, n_i):
    n_q, n_g, sub, n_l = ints.shape
    n_c = n_g // 2
    n_m = n_g * sub
    n_p = weights.shape[1]
    n_di = c_cat.shape[1]
    n_v = n_di // LANES
    n_d = n_aux
    pad_q = (n_q // Q_TILE) * LANES
    n_t = n_q // Q_TILE
    n_rows = n_i * 2 * sub
    half_rows = n_rows // 2
    share = half_rows // n_orb
    units = 2 * n_c
    slots = 4
    n_col = n_l // n_aux
    m_rows = pad_q // n_orb
    own_at = (n_aux - 1) * pad_q
    n_g_rows = pick.shape[0]

    def kernel(b_ref, c_ref, crow_ref, pick_ref, w_hbm, t_ref, mine_ref, j_ref,
               b_buf, w_ref, t_buf, temp, acc, send, part, got, fit, out, g_send, g_got, f_send, f_got, w_vec, w_smem, j_send, j_got,
               y_send, y_recv, x_send, x_recv, gx_send, gx_recv, gy_send, gy_recv, my_send, my_recv, mx_send, mx_recv,
               jy_send, jy_recv, loc, keep):
        j, k = lax.axis_index('aux'), lax.axis_index('orb')
        load_w = pltpu.make_async_copy(w_hbm, w_ref.at[pl.ds(own_at, w_hbm.shape[0])], loc.at[1])

        def load_b(c):
            return pltpu.make_async_copy(b_ref.at[:, pl.ds(2 * c, 2)], b_buf, loc.at[0])

        load_b(0).start()
        load_w.start()
        barrier = pltpu.get_barrier_semaphore()
        for r in range(1, n_aux):
            pl.semaphore_signal(barrier, inc=1, device_id={'aux': lax.rem(j + r, n_aux)}, device_id_type=MESH)
        for r in range(1, n_orb):
            pl.semaphore_signal(barrier, inc=1, device_id={'orb': lax.rem(k + r, n_orb)}, device_id_type=MESH)

        def cut(c, piece):
            if c == 0:
                return slice(None), pl.ds(piece * LANES, LANES)
            return pl.ds(piece * half_rows, half_rows), slice(None)

        def y_copy(c, r, piece):
            to = lax.rem(j + n_aux - r, n_aux)
            rows, lanes = cut(c, piece)
            return pltpu.make_async_remote_copy(
                src_ref=send.at[c % 2, to, rows, lanes], dst_ref=got.at[c, r - 1, rows, lanes], send_sem=y_send.at[c, r - 1, piece],
                recv_sem=y_recv.at[c, r - 1, piece], device_id={'aux': to}, device_id_type=MESH)

        def pieces(c):
            return range(n_t if c == 0 else 2)

        def x_copy(u, r):
            to = lax.rem(k + r, n_orb)
            return pltpu.make_async_remote_copy(
                src_ref=out.at[u % slots, to], dst_ref=t_ref.at[k, u], send_sem=x_send.at[u, r - 1],
                recv_sem=x_recv.at[u, r - 1], device_id={'orb': to}, device_id_type=MESH)

        def my_copy(r):
            to = lax.rem(j + n_aux - r, n_aux)
            return pltpu.make_async_remote_copy(
                src_ref=w_hbm.at[pl.ds(pl.multiple_of(k * m_rows, m_rows), m_rows)],
                dst_ref=w_ref.at[pl.ds(pl.multiple_of((r - 1) * pad_q + k * m_rows, m_rows), m_rows)],
                send_sem=my_send.at[r - 1], recv_sem=my_recv.at[r - 1], device_id={'aux': to}, device_id_type=MESH)

        def mx_copy(r, o):
            rows = w_ref.at[pl.ds(pl.multiple_of((r - 1) * pad_q + k * m_rows, m_rows), m_rows)]
            return pltpu.make_async_remote_copy(
                src_ref=rows, dst_ref=rows, send_sem=mx_send.at[r - 1, o - 1], recv_sem=mx_recv.at[r - 1, o - 1],
                device_id={'orb': lax.rem(k + o, n_orb)}, device_id_type=MESH)

        def jy_copy(r):
            to = lax.rem(j + n_aux - r, n_aux)
            return pltpu.make_async_remote_copy(
                src_ref=j_send.at[to], dst_ref=j_got.at[r - 1], send_sem=jy_send.at[r - 1], recv_sem=jy_recv.at[r - 1],
                device_id={'aux': to}, device_id_type=MESH)

        def gx_copy(r):
            return pltpu.make_async_remote_copy(
                src_ref=g_send, dst_ref=g_got.at[r - 1], send_sem=gx_send.at[r - 1], recv_sem=gx_recv.at[r - 1],
                device_id={'orb': lax.rem(k + r, n_orb)}, device_id_type=MESH)

        def gy_copy(r):
            return pltpu.make_async_remote_copy(
                src_ref=f_send, dst_ref=f_got.at[r - 1], send_sem=gy_send.at[r - 1], recv_sem=gy_recv.at[r - 1],
                device_id={'aux': lax.rem(j + r, n_aux)}, device_id_type=MESH)

        def keep_copies(u):
            return (pltpu.make_async_copy(fit.at[k], mine_ref.at[u], keep.at[0]),
                    pltpu.make_async_copy(out.at[u % slots, k], t_ref.at[k, u], keep.at[1]))

        acc[...] = jnp.zeros_like(acc)
        t_buf[:, Q_TILE * sub:, :] = jnp.zeros((n_v, (LANES - Q_TILE) * sub, LANES), F32)

        def transform(c):
            load_b(c).wait()
            if c >= 2:
                for r in range(1, n_aux):
                    for piece in pieces(c - 2):
                        y_copy(c - 2, r, piece).wait_send()

            def q_tile(t):
                lanes = pl.ds(pl.multiple_of(t * LANES, LANES), LANES)

                @pl.loop(0, 2)
                def _(h):
                    q_rows = pl.ds(pl.multiple_of(t * Q_TILE, Q_TILE), Q_TILE)
                    hi, mid, low = parts3(b_buf[q_rows, h, :, :].reshape(Q_TILE * sub, n_l))
                    left = jnp.concatenate([hi, hi, hi, mid, mid, low], axis=1)
                    res = jnp.dot(left, c_ref[...], preferred_element_type=F32)
                    for v in range(n_v):
                        t_buf[v, 0:Q_TILE * sub, :] = res[:, v * LANES:(v + 1) * LANES]
                    for v in range(n_v):
                        part_di = slice(v * LANES, (v + 1) * LANES)
                        c_row = crow_ref[2 * c + h, :, part_di]
                        live = min(LANES, n_d * n_i - v * LANES)
                        total = acc[t, :, part_di]
                        for m in range(sub):
                            row = t_buf[v, pl.ds(m, LANES, stride=sub), :]
                            total += row * c_row[m:m + 1, :]
                            temp[h, pl.ds(v * LANES * sub + m, live, stride=sub), :] = row.T[:live, :]
                        acc[t, :, part_di] = total

                for d in range(n_d):
                    rows = pl.ds(d * n_i * sub, n_i * sub)
                    both = jnp.concatenate([temp[h, rows, :].reshape(n_i, sub, LANES) for h in range(2)], axis=1)
                    send[c % 2, d, :, lanes] = both.reshape(n_rows, LANES).astype(BF16)
                rows = pl.ds(pl.multiple_of(j * (n_i * sub), n_i * sub), n_i * sub)
                both = jnp.concatenate([temp[h, rows, :].reshape(n_i, sub, LANES) for h in range(2)], axis=1)
                for p, piece in enumerate(parts3(both.reshape(n_rows, LANES))):
                    part[c % 2, :, pl.ds(pl.multiple_of(p * pad_q + t * LANES, LANES), LANES)] = piece

            if c == 0:
                for t in range(n_t):
                    q_tile(t)
                    for r in range(1, n_aux):
                        y_copy(c, r, t).start()
            else:
                pl.loop(0, n_t)(q_tile)
                for piece in pieces(c):
                    for r in range(1, n_aux):
                        y_copy(c, r, piece).start()
            if c + 1 < n_c:
                load_b(c + 1).start()

        def fit_chunk(c):
            for h in range(2):
                u = 2 * c + h
                for piece in (pieces(c) if h == 0 else ()) if c == 0 else (h,):
                    for r in range(1, n_aux):
                        y_copy(c, r, piece).wait_recv()
                if u > 0:
                    for copy in keep_copies(u - 1):
                        copy.wait()
                if u >= slots:
                    for r in range(1, n_orb):
                        x_copy(u - slots, r).wait_send()

                def tile(start, width):
                    rows = slice(h * half_rows, (h + 1) * half_rows)
                    cols = pl.ds(start, width)
                    hi, mid, low = [part[c % 2, rows, p * pad_q:(p + 1) * pad_q] for p in range(3)]
                    left = jnp.concatenate([got[c, r, rows, :] for r in range(n_aux - 1)] + [hi, hi, hi, mid, mid, low], axis=1)
                    res = jnp.dot(left, w_ref[:, cols], preferred_element_type=F32).reshape(n_orb, share, width)
                    out[u % slots, :, :, cols] = res.astype(BF16)
                    fit[:, :, cols] = res

                @pl.loop(0, n_p // WIDE)
                def _(n):
                    tile(pl.multiple_of(n * WIDE, WIDE), WIDE)
                if n_p % WIDE:
                    tile(n_p // WIDE * WIDE, n_p % WIDE)

                for r in range(1, n_orb):
                    x_copy(u, r).start()
                for copy in keep_copies(u):
                    copy.start()

        nt = (((1,), (1,)), ((), ()))
        pl.semaphore_wait(barrier, n_aux + n_orb - 2)
        for r in range(1, n_aux):
            my_copy(r).start()
        transform(0)
        for r in range(1, n_aux):
            my_copy(r).wait_recv()
            for o in range(1, n_orb):
                mx_copy(r, o).start()
        transform(1)
        load_w.wait()
        for r in range(1, n_aux):
            for o in range(1, n_orb):
                mx_copy(r, o).wait_recv()
        fit_chunk(0)
        transform(2)
        load_b(0).start()
        g_send[...] = lax.dot_general(pick_ref[...], acc[...].reshape(n_t * LANES, n_di), nt, precision=PRECISE, preferred_element_type=F32)
        for r in range(1, n_orb):
            gx_copy(r).start()
        fit_chunk(1)
        for r in range(1, n_orb):
            gx_copy(r).wait()
        gamma = g_send[...]
        for r in range(1, n_orb):
            gamma += g_got[r - 1]
        hi, mid, low = parts3(gamma)
        left = jnp.concatenate([hi, hi, hi, mid, mid, low], axis=1)
        f_send[...] = jnp.dot(left, w_ref[own_at:, :], preferred_element_type=F32)
        for r in range(1, n_aux):
            gy_copy(r).start()
        for r in range(1, n_aux):
            gy_copy(r).wait()
        gamma_fit = f_send[...]
        for r in range(1, n_aux):
            gamma_fit += f_got[r - 1]
        hi, mid, low = parts3(gamma_fit)
        m_hi, m_mid, m_low = [w_ref[own_at + p * pad_q:own_at + (p + 1) * pad_q, :] for p in range(3)]
        by_hi = lax.dot_general(jnp.concatenate([hi, mid, low], axis=0), m_hi, nt, preferred_element_type=F32)
        by_mid = lax.dot_general(jnp.concatenate([hi, mid], axis=0), m_mid, nt, preferred_element_type=F32)
        by_low = lax.dot_general(hi, m_low, nt, preferred_element_type=F32)
        n = n_g_rows
        small = by_low + by_mid[n:] + by_hi[2 * n:]
        w_vec[...] = by_hi[:n] + ((by_hi[n:2 * n] + by_mid[:n]) + small)
        to_smem = pltpu.make_async_copy(w_vec, w_smem, loc.at[2])
        to_smem.start()
        to_smem.wait()
        for c in range(n_c):
            load_b(c).wait()
            for h in range(2):
                total = [jnp.zeros((sub, n_l), F32) for _ in range(n_d)]
                for t in range(n_t):
                    def some(s, total):
                        total = list(total)
                        for u in range(8):
                            q = s * 8 + u
                            block = b_buf[t * Q_TILE + q, h]
                            for d in range(n_d):
                                total[d] = total[d] + block * w_smem[d, t * LANES + q]
                        return tuple(total)
                    total = lax.fori_loop(0, Q_TILE // 8, some, tuple(total))
                for d in range(n_d):
                    for to in range(n_aux):
                        j_send[to, d, (2 * c + h) * sub:(2 * c + h + 1) * sub, :] = total[d][:, to * n_col:(to + 1) * n_col]
            if c + 1 < n_c:
                load_b(c + 1).start()
        for r in range(1, n_aux):
            jy_copy(r).start()
        fit_chunk(2)
        for r in range(1, n_aux):
            jy_copy(r).wait()
        coul = j_send[j]
        for r in range(1, n_aux):
            coul += j_got[r - 1]
        j_ref[...] = coul

        for copy in keep_copies(units - 1):
            copy.wait()
        for r in range(1, n_aux):
            my_copy(r).wait_send()
            for o in range(1, n_orb):
                mx_copy(r, o).wait_send()
            for c in range(n_c - 2, n_c):
                for piece in pieces(c):
                    y_copy(c, r, piece).wait_send()
        for u in range(units):
            for r in range(1, n_orb):
                if u >= units - slots:
                    x_copy(u, r).wait_send()
                x_copy(u, r).wait_recv()

    any_spec = pl.BlockSpec(memory_space=pl.ANY)
    vmem = pl.BlockSpec(memory_space=pltpu.VMEM)
    dma = pltpu.SemaphoreType.DMA
    return pl.pallas_call(
        kernel,
        out_shape=(jax.ShapeDtypeStruct((n_orb, units, share, n_p), BF16), jax.ShapeDtypeStruct((units, share, n_p), F32),
                   jax.ShapeDtypeStruct((n_d, n_m, n_col), F32)),
        in_specs=[any_spec, vmem, vmem, vmem, any_spec],
        out_specs=(any_spec, any_spec, vmem),
        scratch_shapes=[
            pltpu.VMEM((n_q, 2, sub, n_l), F32),
            pltpu.VMEM((own_at + weights.shape[0], n_p), BF16),
            pltpu.VMEM((n_v, LANES * sub, LANES), F32),
            pltpu.VMEM((2, n_d * n_i * sub, LANES), F32),
            pltpu.VMEM((n_t, LANES, n_di), F32),
            pltpu.VMEM((2, n_d, n_rows, pad_q), BF16),
            pltpu.VMEM((2, n_rows, 3 * pad_q), BF16),
            pltpu.VMEM((n_c, n_aux - 1, n_rows, pad_q), BF16),
            pltpu.VMEM((n_orb, share, n_p), F32),
            pltpu.VMEM((slots, n_orb, share, n_p), BF16),
            pltpu.VMEM((n_g_rows, pad_q), F32), pltpu.VMEM((n_orb - 1, n_g_rows, pad_q), F32),
            pltpu.VMEM((n_g_rows, n_p), F32), pltpu.VMEM((n_aux - 1, n_g_rows, n_p), F32),
            pltpu.VMEM((n_g_rows, pad_q), F32), pltpu.SMEM((n_g_rows, pad_q), F32),
            pltpu.VMEM((n_aux, n_d, n_m, n_col), F32), pltpu.VMEM((n_aux - 1, n_d, n_m, n_col), F32),
            dma((n_c, n_aux - 1, n_t)), dma((n_c, n_aux - 1, n_t)), dma((units, n_orb - 1)), dma((units, n_orb - 1)),
            dma((n_orb - 1,)), dma((n_orb - 1,)), dma((n_aux - 1,)), dma((n_aux - 1,)),
            dma((n_aux - 1,)), dma((n_aux - 1,)), dma((n_aux - 1, n_orb - 1)), dma((n_aux - 1, n_orb - 1)),
            dma((n_aux - 1,)), dma((n_aux - 1,)),
            dma((3,)), dma((2,)),
        ],
        compiler_params=pltpu.CompilerParams(collective_id=0, has_side_effects=True, vmem_limit_bytes=67043328),
    )(ints, c_cat, c_rows, pick, weights)


def gram(t, mine, coul, n_aux):
    n_k, n_c, n_i, n_r, n_p = t.shape
    n_m, n_n = n_c * n_r, n_k * n_c * n_r
    n_col = n_n // n_aux

    def kernel(t_hbm, mine_ref, coul_ref, g_ref, t_ref, acc, sq, side, k_send, k_got, c_send, c_got,
               load, ks_send, ks_recv, cs_send, cs_recv):
        j, k = lax.axis_index('aux'), lax.axis_index('orb')

        def load_t(i):
            return pltpu.make_async_copy(t_hbm.at[:, :, i], t_ref.at[i], load.at[i])

        def k_copy(r):
            to = lax.rem(k + r, n_k)
            return pltpu.make_async_remote_copy(
                src_ref=k_send.at[to], dst_ref=k_got.at[r - 1], send_sem=ks_send.at[r - 1], recv_sem=ks_recv.at[r - 1],
                device_id={'orb': to}, device_id_type=MESH)

        def c_copy(r):
            to = lax.rem(j + n_aux - r, n_aux)
            return pltpu.make_async_remote_copy(
                src_ref=c_send.at[to], dst_ref=c_got.at[r - 1], send_sem=cs_send.at[r - 1], recv_sem=cs_recv.at[r - 1],
                device_id={'aux': to}, device_id_type=MESH)

        for i in range(n_i):
            load_t(i).start()
        barrier = pltpu.get_barrier_semaphore()
        for r in range(1, n_aux):
            pl.semaphore_signal(barrier, inc=1, device_id={'aux': lax.rem(j + r, n_aux)}, device_id_type=MESH)
        for r in range(1, n_k):
            pl.semaphore_signal(barrier, inc=1, device_id={'orb': lax.rem(k + r, n_k)}, device_id_type=MESH)
        acc[...] = jnp.zeros_like(acc)
        sq[...] = jnp.zeros_like(sq)
        nt = (((1,), (1,)), ((), ()))

        @pl.loop(0, n_i)
        def _(i):
            load_t(i).wait()
            all_t = t_ref[i].reshape(n_n, n_p)
            own = mine_ref[:, i].reshape(n_m, n_p)
            _, mid, low = parts3(own)
            left = jnp.concatenate([all_t, mid, low], axis=0)
            acc[...] += lax.dot_general(left, all_t, nt, preferred_element_type=F32)
            sq[...] += lax.dot_general(mid, mid, nt, preferred_element_type=F32)

        put = lax.broadcasted_iota(jnp.int32, (n_m, n_n), 1) == lax.broadcasted_iota(jnp.int32, (n_m, n_n), 0) + k * n_m
        own_sq = jnp.dot(0.5 * sq[...], put.astype(F32), precision=PRECISE, preferred_element_type=F32)
        side[...] = jnp.zeros_like(side)
        side[pl.ds(pl.multiple_of(k * n_m, 8), n_m), :] = acc[n_n:n_n + n_m, :] + acc[n_n + n_m:, :] + own_sq
        k_send[...] = (acc[:n_n, :] + side[...] + side[...].T).reshape(n_k, n_m, n_n)
        pl.semaphore_wait(barrier, n_aux + n_k - 2)
        for r in range(1, n_k):
            k_copy(r).start()
        for r in range(1, n_k):
            k_copy(r).wait()
        total = k_send[k]
        for r in range(1, n_k):
            total += k_got[r - 1]
        for to in range(n_aux):
            c_send[to] = total[:, to * n_col:(to + 1) * n_col]
        for r in range(1, n_aux):
            c_copy(r).start()
        g_ref[j] = 2.0 * coul_ref[j] - c_send[j]
        for r in range(1, n_aux):
            c_copy(r).wait()
            d = lax.rem(j + r, n_aux)
            g_ref[d] = 2.0 * coul_ref[d] - c_got[r - 1]

    any_spec = pl.BlockSpec(memory_space=pl.ANY)
    vmem = pl.BlockSpec(memory_space=pltpu.VMEM)
    dma = pltpu.SemaphoreType.DMA
    return pl.pallas_call(
        kernel,
        out_shape=jax.ShapeDtypeStruct((n_aux, n_m, n_col), F32),
        in_specs=[any_spec, vmem, vmem],
        out_specs=vmem,
        scratch_shapes=[
            pltpu.VMEM((n_i, n_k, n_c, n_r, n_p), BF16),
            pltpu.VMEM((n_n + 2 * n_m, n_n), F32), pltpu.VMEM((n_m, n_m), F32), pltpu.VMEM((n_n, n_n), F32),
            pltpu.VMEM((n_k, n_m, n_n), F32), pltpu.VMEM((n_k - 1, n_m, n_n), F32),
            pltpu.VMEM((n_aux, n_m, n_col), F32), pltpu.VMEM((n_aux - 1, n_m, n_col), F32),
            dma((n_i,)), dma((n_k - 1,)), dma((n_k - 1,)), dma((n_aux - 1,)), dma((n_aux - 1,)),
        ],
        compiler_params=pltpu.CompilerParams(collective_id=1, has_side_effects=True, vmem_limit_bytes=40 * 2**20),
    )(t, mine, coul)


def solution(mesh):
    n_aux, n_orb = mesh.shape['aux'], mesh.shape['orb']

    def local_fock(ints, metric, orbitals):
        n_q, n_m, n_l = ints.shape
        n_d, _, n_i = orbitals.shape
        n_p = n_aux * n_q
        n_c = n_m // (2 * SUB)
        pad_p = round_up(n_p, LANES)
        n_t = n_q // Q_TILE
        pad_q = n_t * LANES
        pad_di = round_up(n_d * n_i, LANES)
        k = lax.axis_index('orb')

        metric_pad = jnp.pad(metric.reshape(n_t, Q_TILE, n_p), ((0, 0), (0, LANES - Q_TILE), (0, pad_p - n_p))).reshape(pad_q, pad_p)
        m_hi, m_mid, m_low = split3(metric_pad)
        fit_w = jnp.concatenate([m_hi, m_mid, m_low, m_hi, m_mid, m_hi], axis=0)

        c_all = jnp.pad(orbitals.transpose(1, 0, 2).reshape(n_l, n_d * n_i), ((0, 0), (0, pad_di - n_d * n_i)))
        c_hi, c_mid, c_low = split3(c_all)
        c_cat = jnp.concatenate([c_hi, c_mid, c_low, c_hi, c_mid, c_hi], axis=0)
        c_rows = lax.dynamic_slice_in_dim(c_all, k * n_m, n_m, axis=0)
        lane = jnp.arange(pad_di)[None, :] // n_i
        pick = (lane == jnp.arange(2 * SUB)[:, None]).astype(F32)
        all_t, mine, coul = fit_exchange(ints.reshape(n_q, n_m // SUB, SUB, n_l), c_cat, c_rows.reshape(n_m // SUB, SUB, pad_di), pick, fit_w, n_aux, n_orb, n_i)
        all_t = all_t.reshape(n_orb, n_c, n_i // n_orb, 2 * SUB, pad_p)
        mine = mine.reshape(n_c, n_i // n_orb, 2 * SUB, pad_p)
        return gram(all_t, mine, coul, n_aux)

    return jax.shard_map(local_fock, mesh=mesh, in_specs=(P(('sys', 'aux'), 'orb', None), P(('sys', 'aux'), None), P('sys', None, None)), out_specs=P('sys', 'orb', 'aux'), check_vma=False)
```

time: 379 us -> 265 us (0.70)
  waiting for transfers between devices: 84.5 us -> 0 us
  between operations: 13.4 us -> 0.05 us
  starting transfers between devices: 4.52 us -> 0 us
  other arithmetic: 9.95 us -> 5.78 us
    all_gather x1 -> x0, waiting for transfers between devices: 46.9 us -> none  [local_fock(): met = lax.all_gather(m_hi, 'aux', axis=0)]
    reduce_scatter x1 -> x0, waiting for transfers between devices: 23.2 us -> none  [local_fock(): exch = lax.psum_scatter(exch, 'orb', scatter_dimension=0, tiled=True)]
    unnamed x4 -> x0, waiting for transfers between devices: 14.4 us -> none
    all_to_all x1 -> x0, starting transfers between devices: 4.39 us -> none  [local_fock(): exch = lax.all_to_all(exch.reshape(n_m, n_aux, n_n // n_aux), 'aux', 1, 0)]
    unnamed x24 -> x14, local copies, waits for them, and re-layouts: 14 us -> 12.8 us
  transfers between devices with their start and end apart: 4 -> 0, of which waited for: 3 -> 0; matrix products, arithmetic and copies ran while one was open for 2% -> 0% of each run, Pallas kernels for 0% -> 0%
where the time goes in v1:
time: 265 us; the launch traced here: 264 us
  Pallas kernels  243 us (92%)
  local copies, waits for them, and re-layouts  15.9 us (6%)
  other arithmetic  5.78 us (2%)
    pallas_call x1, Pallas kernels, fit_exchange(): pl.pallas_call(kernel, out_shape=(jax.ShapeDtypeStruct((n_orb, units, sha...  221 us
    pallas_call x1, Pallas kernels, gram(): pl.pallas_call(kernel, out_shape=jax.ShapeDtypeStruct((n_aux, n_m, n_col)...  21.9 us
    unnamed x14, local copies, waits for them, and re-layouts  12.8 us

profile of v1, /device:TPU:97, one launch (start us, length us, event | category | flops | bytes accessed | tf_op | source)
XLA Modules:
  0.0 264.3 jit_solution(14559100657399291229)
XLA Ops:
  0.0 0.6 fusion.4.pick_ref
  0.6 1.3 copy.5
  1.9 0.6 fusion.3.crow_ref
  2.5 0.7 constant_dynamic-update-slice_fusion.4
  3.3 0.8 constant_dynamic-update-slice_fusion.3
  4.1 0.0 copy-start.3
  4.1 0.8 fusion.2
  4.9 0.7 constant_dynamic-update-slice_fusion.2
  5.6 0.8 constant_dynamic-update-slice_fusion.1
  6.4 0.8 constant_dynamic-update-slice_fusion.c_ref
  7.2 0.0 copy-done.3
  7.2 0.1 pad.9
  7.4 0.5 fusion
  7.8 1.1 constant_dynamic-update-slice_fusion.10
  8.9 1.1 constant_dynamic-update-slice_fusion.9
  10.0 1.1 constant_dynamic-update-slice_fusion.8
  11.1 1.1 constant_dynamic-update-slice_fusion.7
  12.2 1.1 constant_dynamic-update-slice_fusion.6
  13.3 1.1 constant_dynamic-update-slice_fusion.5.w_hbm
  14.3 220.6 %shard_map.37 = (bf16[8,6,80,1408]{3,2,1,0:T(8,128)(2,1)}, f32[6,80,1408]{2,1,0:T(8,128)}, f32[4,48,96]{2,1,0:T(8,128)}) custom-call(f32[336,6,8,384]{3,2,1,0:T(8,128)} %bitcast.18, bf16[2304,384]{1,0:T(8,128)(2,1)} %constant_dynamic-update-slice_fusion.c_ref, f32[6,8,384]{2,1,0:T(8,128)} %fusion.3.crow_ref, f32[16,384]{1,0:T(8,128)} %fusion.4.pick_ref, ...), custom_call_target="tpu_custom_call" | custom-call | tf_op jit(solution)/shard_map/pallas_call | solution.py:308
  234.9 0.0 copy-start
  235.0 4.1 %copy-done = bf16[8,6,80,1408]{3,2,1,0:T(8,128)(2,1)S(1)} copy-done((bf16[8,6,80,1408]{3,2,1,0:T(8,128)(2,1)S(1)}, bf16[8,6,80,1408]{3,2,1,0:T(8,128)(2,1)}, u32[]{:S(2)}) %copy-start) | copy-done | bytes 10813464
  239.0 0.0 copy-start.1
  239.0 1.8 copy-done.1
  240.8 0.0 copy-start.2
  240.8 0.9 copy-done.2
  241.7 21.9 %shard_map.38 = f32[4,48,96]{2,1,0:T(8,128)S(1)} custom-call(bf16[8,3,10,16,1408]{4,3,2,1,0:T(8,128)(2,1)S(1)} %bitcast.16, f32[3,10,16,1408]{3,2,1,0:T(8,128)S(1)} %bitcast.17, f32[4,48,96]{2,1,0:T(8,128)S(1)} %copy-done.2), custom_call_target="tpu_custom_call" | custom-call | tf_op jit(solution)/shard_map/pallas_call | solution.py:410
  263.6 0.6 copy.17
  (1 shorter events, 0.0 us)
Async XLA Ops:
  4.1 3.1 %copy-start.3 = (f32[336,1344]{1,0:T(8,128)S(1)}, f32[336,1344]{1,0:T(8,128)}, u32[]{:S(2)}) copy-start(f32[336,1344]{1,0:T(8,128)} %param.4) | copy-start | bytes 5419012
  234.9 4.1 %copy-start = (bf16[8,6,80,1408]{3,2,1,0:T(8,128)(2,1)S(1)}, bf16[8,6,80,1408]{3,2,1,0:T(8,128)(2,1)}, u32[]{:S(2)}) copy-start(bf16[8,6,80,1408]{3,2,1,0:T(8,128)(2,1)} %get-tuple-element.8) | copy-start | bytes 32440324
  239.0 1.8 copy-start.1
  240.8 0.9 copy-start.2

commit v2 on v1

--- a/solution.py
+++ b/solution.py
@@ -71,8 +71,8 @@
             pl.semaphore_signal(barrier, inc=1, device_id={'orb': lax.rem(k + r, n_orb)}, device_id_type=MESH)
 
         def cut(c, piece):
-            if c == 0:
-                return slice(None), pl.ds(piece * LANES, LANES)
+            if piece >= 2:
+                return pl.ds(0, half_rows), pl.ds((piece - 2) * LANES, LANES)
             return pl.ds(piece * half_rows, half_rows), slice(None)
 
         def y_copy(c, r, piece):
@@ -82,8 +82,8 @@
                 src_ref=send.at[c % 2, to, rows, lanes], dst_ref=got.at[c, r - 1, rows, lanes], send_sem=y_send.at[c, r - 1, piece],
                 recv_sem=y_recv.at[c, r - 1, piece], device_id={'aux': to}, device_id_type=MESH)
 
-        def pieces(c):
-            return range(n_t if c == 0 else 2)
+        def pieces(c, h):
+            return tuple(range(2, 2 + n_t)) if c == 0 and h == 0 else (h,)
 
         def x_copy(u, r):
             to = lax.rem(k + r, n_orb)
@@ -131,7 +131,7 @@
             load_b(c).wait()
             if c >= 2:
                 for r in range(1, n_aux):
-                    for piece in pieces(c - 2):
+                    for piece in pieces(c - 2, 0) + pieces(c - 2, 1):
                         y_copy(c - 2, r, piece).wait_send()
 
             def q_tile(t):
@@ -169,69 +169,72 @@
                 for t in range(n_t):
                     q_tile(t)
                     for r in range(1, n_aux):
-                        y_copy(c, r, t).start()
+                        y_copy(c, r, 2 + t).start()
+                    if t == 0:
+                        for r in range(1, n_aux):
+                            my_copy(r).wait_recv()
+                            for o in range(1, n_orb):
+                                mx_copy(r, o).start()
+                for r in range(1, n_aux):
+                    y_copy(c, r, 1).start()
             else:
                 pl.loop(0, n_t)(q_tile)
-                for piece in pieces(c):
+                for piece in (0, 1):
                     for r in range(1, n_aux):
                         y_copy(c, r, piece).start()
             if c + 1 < n_c:
                 load_b(c + 1).start()
 
-        def fit_chunk(c):
-            for h in range(2):
-                u = 2 * c + h
-                for piece in (pieces(c) if h == 0 else ()) if c == 0 else (h,):
-                    for r in range(1, n_aux):
-                        y_copy(c, r, piece).wait_recv()
-                if u > 0:
-                    for copy in keep_copies(u - 1):
-                        copy.wait()
-                if u >= slots:
-                    for r in range(1, n_orb):
-                        x_copy(u - slots, r).wait_send()
-
-                def tile(start, width):
-                    rows = slice(h * half_rows, (h + 1) * half_rows)
-                    cols = pl.ds(start, width)
-                    hi, mid, low = [part[c % 2, rows, p * pad_q:(p + 1) * pad_q] for p in range(3)]
-                    left = jnp.concatenate([got[c, r, rows, :] for r in range(n_aux - 1)] + [hi, hi, hi, mid, mid, low], axis=1)
-                    res = jnp.dot(left, w_ref[:, cols], preferred_element_type=F32).reshape(n_orb, share, width)
-                    out[u % slots, :, :, cols] = res.astype(BF16)
-                    fit[:, :, cols] = res
-
-                @pl.loop(0, n_p // WIDE)
-                def _(n):
-                    tile(pl.multiple_of(n * WIDE, WIDE), WIDE)
-                if n_p % WIDE:
-                    tile(n_p // WIDE * WIDE, n_p % WIDE)
-
+        def fit_half(c, h):
+            u = 2 * c + h
+            for piece in pieces(c, h):
+                for r in range(1, n_aux):
+                    y_copy(c, r, piece).wait_recv()
+            if u > 0:
+                for copy in keep_copies(u - 1):
+                    copy.wait()
+            if u >= slots:
                 for r in range(1, n_orb):
-                    x_copy(u, r).start()
-                for copy in keep_copies(u):
-                    copy.start()
+                    x_copy(u - slots, r).wait_send()
+
+            def tile(start, width):
+                rows = slice(h * half_rows, (h + 1) * half_rows)
+                cols = pl.ds(start, width)
+                hi, mid, low = [part[c % 2, rows, p * pad_q:(p + 1) * pad_q] for p in range(3)]
+                left = jnp.concatenate([got[c, r, rows, :] for r in range(n_aux - 1)] + [hi, hi, hi, mid, mid, low], axis=1)
+                res = jnp.dot(left, w_ref[:, cols], preferred_element_type=F32).reshape(n_orb, share, width)
+                out[u % slots, :, :, cols] = res.astype(BF16)
+                fit[:, :, cols] = res
+
+            @pl.loop(0, n_p // WIDE)
+            def _(n):
+                tile(pl.multiple_of(n * WIDE, WIDE), WIDE)
+            if n_p % WIDE:
+                tile(n_p // WIDE * WIDE, n_p % WIDE)
+
+            for r in range(1, n_orb):
+                x_copy(u, r).start()
+            for copy in keep_copies(u):
+                copy.start()
 
         nt = (((1,), (1,)), ((), ()))
         pl.semaphore_wait(barrier, n_aux + n_orb - 2)
         for r in range(1, n_aux):
             my_copy(r).start()
         transform(0)
-        for r in range(1, n_aux):
-            my_copy(r).wait_recv()
-            for o in range(1, n_orb):
-                mx_copy(r, o).start()
         transform(1)
         load_w.wait()
         for r in range(1, n_aux):
             for o in range(1, n_orb):
                 mx_copy(r, o).wait_recv()
-        fit_chunk(0)
+        fit_half(0, 0)
+        fit_half(0, 1)
         transform(2)
         load_b(0).start()
         g_send[...] = lax.dot_general(pick_ref[...], acc[...].reshape(n_t * LANES, n_di), nt, precision=PRECISE, preferred_element_type=F32)
         for r in range(1, n_orb):
             gx_copy(r).start()
-        fit_chunk(1)
+        fit_half(1, 0)
         for r in range(1, n_orb):
             gx_copy(r).wait()
         gamma = g_send[...]
@@ -242,6 +245,7 @@
         f_send[...] = jnp.dot(left, w_ref[own_at:, :], preferred_element_type=F32)
         for r in range(1, n_aux):
             gy_copy(r).start()
+        fit_half(1, 1)
         for r in range(1, n_aux):
             gy_copy(r).wait()
         gamma_fit = f_send[...]
@@ -259,6 +263,8 @@
         to_smem.start()
         to_smem.wait()
         for c in range(n_c):
+            if c > 0:
+                fit_half(2, c - 1)
             load_b(c).wait()
             for h in range(2):
                 total = [jnp.zeros((sub, n_l), F32) for _ in range(n_d)]
@@ -279,7 +285,6 @@
                 load_b(c + 1).start()
         for r in range(1, n_aux):
             jy_copy(r).start()
-        fit_chunk(2)
         for r in range(1, n_aux):
             jy_copy(r).wait()
         coul = j_send[j]
@@ -294,7 +299,7 @@
             for o in range(1, n_orb):
                 mx_copy(r, o).wait_send()
             for c in range(n_c - 2, n_c):
-                for piece in pieces(c):
+                for piece in pieces(c, 0) + pieces(c, 1):
                     y_copy(c, r, piece).wait_send()
         for u in range(units):
             for r in range(1, n_orb):
@@ -326,7 +331,7 @@
             pltpu.VMEM((n_g_rows, n_p), F32), pltpu.VMEM((n_aux - 1, n_g_rows, n_p), F32),
             pltpu.VMEM((n_g_rows, pad_q), F32), pltpu.SMEM((n_g_rows, pad_q), F32),
             pltpu.VMEM((n_aux, n_d, n_m, n_col), F32), pltpu.VMEM((n_aux - 1, n_d, n_m, n_col), F32),
-            dma((n_c, n_aux - 1, n_t)), dma((n_c, n_aux - 1, n_t)), dma((units, n_orb - 1)), dma((units, n_orb - 1)),
+            dma((n_c, n_aux - 1, 2 + n_t)), dma((n_c, n_aux - 1, 2 + n_t)), dma((units, n_orb - 1)), dma((units, n_orb - 1)),
             dma((n_orb - 1,)), dma((n_orb - 1,)), dma((n_aux - 1,)), dma((n_aux - 1,)),
             dma((n_aux - 1,)), dma((n_aux - 1,)), dma((n_aux - 1, n_orb - 1)), dma((n_aux - 1, n_orb - 1)),
             dma((n_aux - 1,)), dma((n_aux - 1,)),
@@ -341,13 +346,16 @@
     n_m, n_n = n_c * n_r, n_k * n_c * n_r
     n_col = n_n // n_aux
 
-    def kernel(t_hbm, mine_ref, coul_ref, g_ref, t_ref, acc, sq, side, k_send, k_got, c_send, c_got,
-               load, ks_send, ks_recv, cs_send, cs_recv):
+    def kernel(t_hbm, mine_hbm, coul_ref, g_ref, t_ref, mine_ref, acc, sq, side, k_send, k_got, c_send, c_got,
+               load, load_m, ks_send, ks_recv, cs_send, cs_recv):
         j, k = lax.axis_index('aux'), lax.axis_index('orb')
 
         def load_t(i):
             return pltpu.make_async_copy(t_hbm.at[:, :, i], t_ref.at[i], load.at[i])
 
+        def load_own(i):
+            return pltpu.make_async_copy(mine_hbm.at[:, i], mine_ref.at[i], load_m.at[i])
+
         def k_copy(r):
             to = lax.rem(k + r, n_k)
             return pltpu.make_async_remote_copy(
@@ -362,6 +370,7 @@
 
         for i in range(n_i):
             load_t(i).start()
+            load_own(i).start()
         barrier = pltpu.get_barrier_semaphore()
         for r in range(1, n_aux):
             pl.semaphore_signal(barrier, inc=1, device_id={'aux': lax.rem(j + r, n_aux)}, device_id_type=MESH)
@@ -374,8 +383,9 @@
         @pl.loop(0, n_i)
         def _(i):
             load_t(i).wait()
+            load_own(i).wait()
             all_t = t_ref[i].reshape(n_n, n_p)
-            own = mine_ref[:, i].reshape(n_m, n_p)
+            own = mine_ref[i].reshape(n_m, n_p)
             _, mid, low = parts3(own)
             left = jnp.concatenate([all_t, mid, low], axis=0)
             acc[...] += lax.dot_general(left, all_t, nt, preferred_element_type=F32)
@@ -410,16 +420,16 @@
     return pl.pallas_call(
         kernel,
         out_shape=jax.ShapeDtypeStruct((n_aux, n_m, n_col), F32),
-        in_specs=[any_spec, vmem, vmem],
+        in_specs=[any_spec, any_spec, vmem],
         out_specs=vmem,
         scratch_shapes=[
-            pltpu.VMEM((n_i, n_k, n_c, n_r, n_p), BF16),
+            pltpu.VMEM((n_i, n_k, n_c, n_r, n_p), BF16), pltpu.VMEM((n_i, n_c, n_r, n_p), F32),
             pltpu.VMEM((n_n + 2 * n_m, n_n), F32), pltpu.VMEM((n_m, n_m), F32), pltpu.VMEM((n_n, n_n), F32),
             pltpu.VMEM((n_k, n_m, n_n), F32), pltpu.VMEM((n_k - 1, n_m, n_n), F32),
             pltpu.VMEM((n_aux, n_m, n_col), F32), pltpu.VMEM((n_aux - 1, n_m, n_col), F32),
-            dma((n_i,)), dma((n_k - 1,)), dma((n_k - 1,)), dma((n_aux - 1,)), dma((n_aux - 1,)),
+            dma((n_i,)), dma((n_i,)), dma((n_k - 1,)), dma((n_k - 1,)), dma((n_aux - 1,)), dma((n_aux - 1,)),
         ],
-        compiler_params=pltpu.CompilerParams(collective_id=1, has_side_effects=True, vmem_limit_bytes=40 * 2**20),
+        compiler_params=pltpu.CompilerParams(collective_id=1, has_side_effects=True, vmem_limit_bytes=67043328),
     )(t, mine, coul)
 
 

time: 265 us -> 248 us (0.936)
  Pallas kernels: 243 us -> 232 us
  local copies, waits for them, and re-layouts: 15.9 us -> 10.1 us
    pallas_call x1, Pallas kernels: 221 us -> 207 us  [fit_exchange(): pl.pallas_call(kernel, out_shape=(jax.ShapeDtypeStruct((n_orb, units, sha...]
    unnamed x14 -> x8, local copies, waits for them, and re-layouts: 12.8 us -> 6.99 us
where the time goes in v2:
time: 248 us
  Pallas kernels  232 us (94%)
  local copies, waits for them, and re-layouts  10.1 us (4%)
  other arithmetic  5.74 us (2%)
    pallas_call x1, Pallas kernels, fit_exchange(): pl.pallas_call(kernel, out_shape=(jax.ShapeDtypeStruct((n_orb, units, sha...  207 us
    pallas_call x1, Pallas kernels, gram(): pl.pallas_call(kernel, out_shape=jax.ShapeDtypeStruct((n_aux, n_m, n_col)...  24.4 us
    unnamed x8, local copies, waits for them, and re-layouts  6.99 us

profile of v2, /device:TPU:97, one launch (start us, length us, event | category | flops | bytes accessed | tf_op | source)
XLA Modules:
  0.0 247.6 jit_solution(17110509306739030370)
XLA Ops:
  0.0 0.6 fusion.4.pick_ref
  0.6 1.3 copy.5
  1.9 0.6 fusion.3.crow_ref
  2.5 0.7 constant_dynamic-update-slice_fusion.4
  3.3 0.8 constant_dynamic-update-slice_fusion.3
  4.1 0.0 copy-start
  4.1 0.8 fusion.2
  4.9 0.7 constant_dynamic-update-slice_fusion.2
  5.6 0.8 constant_dynamic-update-slice_fusion.1
  6.4 0.8 constant_dynamic-update-slice_fusion.c_ref
  7.2 0.0 copy-done
  7.2 0.1 pad.9
  7.3 0.5 fusion
  7.8 1.1 constant_dynamic-update-slice_fusion.10
  8.9 1.1 constant_dynamic-update-slice_fusion.9
  10.0 1.1 constant_dynamic-update-slice_fusion.8
  11.1 1.1 constant_dynamic-update-slice_fusion.7
  12.2 1.1 constant_dynamic-update-slice_fusion.6
  13.3 1.1 constant_dynamic-update-slice_fusion.5.w_hbm
  14.3 207.4 %shard_map.37 = (bf16[8,6,80,1408]{3,2,1,0:T(8,128)(2,1)}, f32[6,80,1408]{2,1,0:T(8,128)}, f32[4,48,96]{2,1,0:T(8,128)}) custom-call(f32[336,6,8,384]{3,2,1,0:T(8,128)} %bitcast.16, bf16[2304,384]{1,0:T(8,128)(2,1)} %constant_dynamic-update-slice_fusion.c_ref, f32[6,8,384]{2,1,0:T(8,128)} %fusion.3.crow_ref, f32[16,384]{1,0:T(8,128)} %fusion.4.pick_ref, ...), custom_call_target="tpu_custom_call" | custom-call | tf_op jit(solution)/shard_map/pallas_call | solution.py:313
  221.7 24.4 %shard_map.38 = f32[4,48,96]{2,1,0:T(8,128)} custom-call(bf16[8,3,10,16,1408]{4,3,2,1,0:T(8,128)(2,1)} %bitcast.17, f32[3,10,16,1408]{3,2,1,0:T(8,128)} %bitcast.18, f32[4,48,96]{2,1,0:T(8,128)} %get-tuple-element.10.coul_ref), custom_call_target="tpu_custom_call" | custom-call | tf_op jit(solution)/shard_map/pallas_call | solution.py:420
  246.1 1.5 copy.17
  (1 shorter events, 0.0 us)
Async XLA Ops:
  4.1 3.1 %copy-start = (f32[336,1344]{1,0:T(8,128)S(1)}, f32[336,1344]{1,0:T(8,128)}, u32[]{:S(2)}) copy-start(f32[336,1344]{1,0:T(8,128)} %param.4) | copy-start | bytes 5419012

commit v3 on v2

--- a/solution.py
+++ b/solution.py
@@ -32,11 +32,12 @@
     return hi.astype(BF16), mid.astype(BF16), (x - hi - mid).astype(BF16)
 
 
-def fit_exchange(ints, c_cat, c_rows, pick, weights, n_aux, n_orb, n_i):
+def fock(ints, c_cat, c_rows, pick, parts, n_aux, n_orb, n_i):
     n_q, n_g, sub, n_l = ints.shape
     n_c = n_g // 2
     n_m = n_g * sub
-    n_p = weights.shape[1]
+    n_p = parts[0].shape[1]
+    order = (0, 1, 2, 0, 1, 0)
     n_di = c_cat.shape[1]
     n_v = n_di // LANES
     n_d = n_aux
@@ -48,22 +49,27 @@
     units = 2 * n_c
     slots = 4
     n_col = n_l // n_aux
+    group = 2 * sub
+    n_ii = share // group
     m_rows = pad_q // n_orb
     own_at = (n_aux - 1) * pad_q
     n_g_rows = pick.shape[0]
 
-    def kernel(b_ref, c_ref, crow_ref, pick_ref, w_hbm, t_ref, mine_ref, j_ref,
-               b_buf, w_ref, t_buf, temp, acc, send, part, got, fit, out, g_send, g_got, f_send, f_got, w_vec, w_smem, j_send, j_got,
+    def kernel(b_ref, c_ref, crow_ref, pick_ref, w_hi, w_mid, w_low, g_ref, t_ref, mine_ref,
+               b_buf, w_ref, t_buf, temp, acc, send, part, got, fit, out, g_send, g_got, f_send, f_got, w_vec, w_smem, j_send, j_got, coul,
                y_send, y_recv, x_send, x_recv, gx_send, gx_recv, gy_send, gy_recv, my_send, my_recv, mx_send, mx_recv,
-               jy_send, jy_recv, loc, keep):
+               jy_send, jy_recv, loc, keep, load, load_w, ks_send, ks_recv, cs_send, cs_recv,
+               t_in, mine_in, prod, sq, side, k_send, k_got, c_send, c_got):
         j, k = lax.axis_index('aux'), lax.axis_index('orb')
-        load_w = pltpu.make_async_copy(w_hbm, w_ref.at[pl.ds(own_at, w_hbm.shape[0])], loc.at[1])
+        w_in = [pltpu.make_async_copy((w_hi, w_mid, w_low)[p], w_ref.at[pl.ds(own_at + n * pad_q, pad_q)], load_w.at[n])
+                for n, p in enumerate(order)]
 
         def load_b(c):
             return pltpu.make_async_copy(b_ref.at[:, pl.ds(2 * c, 2)], b_buf, loc.at[0])
 
         load_b(0).start()
-        load_w.start()
+        for copy in w_in:
+            copy.start()
         barrier = pltpu.get_barrier_semaphore()
         for r in range(1, n_aux):
             pl.semaphore_signal(barrier, inc=1, device_id={'aux': lax.rem(j + r, n_aux)}, device_id_type=MESH)
@@ -94,7 +100,7 @@
         def my_copy(r):
             to = lax.rem(j + n_aux - r, n_aux)
             return pltpu.make_async_remote_copy(
-                src_ref=w_hbm.at[pl.ds(pl.multiple_of(k * m_rows, m_rows), m_rows)],
+                src_ref=w_hi.at[pl.ds(pl.multiple_of(k * m_rows, m_rows), m_rows)],
                 dst_ref=w_ref.at[pl.ds(pl.multiple_of((r - 1) * pad_q + k * m_rows, m_rows), m_rows)],
                 send_sem=my_send.at[r - 1], recv_sem=my_recv.at[r - 1], device_id={'aux': to}, device_id_type=MESH)
 
@@ -121,7 +127,7 @@
                 device_id={'aux': lax.rem(j + r, n_aux)}, device_id_type=MESH)
 
         def keep_copies(u):
-            return (pltpu.make_async_copy(fit.at[k], mine_ref.at[u], keep.at[0]),
+            return (pltpu.make_async_copy(fit, mine_ref.at[u], keep.at[0]),
                     pltpu.make_async_copy(out.at[u % slots, k], t_ref.at[k, u], keep.at[1]))
 
         acc[...] = jnp.zeros_like(acc)
@@ -204,7 +210,10 @@
                 left = jnp.concatenate([got[c, r, rows, :] for r in range(n_aux - 1)] + [hi, hi, hi, mid, mid, low], axis=1)
                 res = jnp.dot(left, w_ref[:, cols], preferred_element_type=F32).reshape(n_orb, share, width)
                 out[u % slots, :, :, cols] = res.astype(BF16)
-                fit[:, :, cols] = res
+                for b in range(n_orb):
+                    @pl.when(k == b)
+                    def _(b=b):
+                        fit[:, cols] = res[b]
 
             @pl.loop(0, n_p // WIDE)
             def _(n):
@@ -223,7 +232,8 @@
             my_copy(r).start()
         transform(0)
         transform(1)
-        load_w.wait()
+        for copy in w_in:
+            copy.wait()
         for r in range(1, n_aux):
             for o in range(1, n_orb):
                 mx_copy(r, o).wait_recv()
@@ -287,13 +297,79 @@
             jy_copy(r).start()
         for r in range(1, n_aux):
             jy_copy(r).wait()
-        coul = j_send[j]
-        for r in range(1, n_aux):
-            coul += j_got[r - 1]
-        j_ref[...] = coul
-
-        for copy in keep_copies(units - 1):
-            copy.wait()
+        coul[...] = j_send[j]
+        for r in range(1, n_aux):
+            coul[...] += j_got[r - 1]
+
+        def t_load(h, i):
+            slot = lax.rem(i, 2)
+            rows = pl.ds(pl.multiple_of(i * group, group), group)
+            return [pltpu.make_async_copy(t_ref.at[:, 2 * c + h, rows], t_in.at[slot, :, c], load.at[slot, c]) for c in range(n_c)] + [
+                pltpu.make_async_copy(mine_ref.at[2 * c + h, rows], mine_in.at[slot, c], load.at[slot, n_c + c]) for c in range(n_c)]
+
+        prod[...] = jnp.zeros_like(prod)
+        sq[...] = jnp.zeros_like(sq)
+        for h in range(2):
+            if h == 1:
+                for copy in keep_copies(units - 1):
+                    copy.wait()
+            for c in range(n_c):
+                for r in range(1, n_orb):
+                    x_copy(2 * c + h, r).wait_recv()
+            for i in range(2):
+                for copy in t_load(h, i):
+                    copy.start()
+
+            @pl.loop(0, n_ii)
+            def _(i):
+                for copy in t_load(h, i):
+                    copy.wait()
+                slot = lax.rem(i, 2)
+                all_t = t_in[slot].reshape(n_l, n_p)
+                _, mid, low = parts3(mine_in[slot].reshape(n_m, n_p))
+                left = jnp.concatenate([all_t, mid, low], axis=0)
+                prod[...] += lax.dot_general(left, all_t, nt, preferred_element_type=F32)
+                sq[...] += lax.dot_general(mid, mid, nt, preferred_element_type=F32)
+
+                @pl.when(i + 2 < n_ii)
+                def _():
+                    for copy in t_load(h, i + 2):
+                        copy.start()
+
+        def k_copy(r):
+            to = lax.rem(k + r, n_orb)
+            return pltpu.make_async_remote_copy(
+                src_ref=k_send.at[to], dst_ref=k_got.at[r - 1], send_sem=ks_send.at[r - 1], recv_sem=ks_recv.at[r - 1],
+                device_id={'orb': to}, device_id_type=MESH)
+
+        def c_copy(r):
+            to = lax.rem(j + n_aux - r, n_aux)
+            return pltpu.make_async_remote_copy(
+                src_ref=c_send.at[to], dst_ref=c_got.at[r - 1], send_sem=cs_send.at[r - 1], recv_sem=cs_recv.at[r - 1],
+                device_id={'aux': to}, device_id_type=MESH)
+
+        put = lax.broadcasted_iota(jnp.int32, (n_m, n_l), 1) == lax.broadcasted_iota(jnp.int32, (n_m, n_l), 0) + k * n_m
+        own_sq = jnp.dot(0.5 * sq[...], put.astype(F32), precision=PRECISE, preferred_element_type=F32)
+        side[...] = jnp.zeros_like(side)
+        side[pl.ds(pl.multiple_of(k * n_m, 8), n_m), :] = prod[n_l:n_l + n_m, :] + prod[n_l + n_m:, :] + own_sq
+        k_send[...] = (prod[:n_l, :] + side[...] + side[...].T).reshape(n_orb, n_m, n_l)
+        for r in range(1, n_orb):
+            k_copy(r).start()
+        for r in range(1, n_orb):
+            k_copy(r).wait()
+        total = k_send[k]
+        for r in range(1, n_orb):
+            total += k_got[r - 1]
+        for to in range(n_aux):
+            c_send[to] = total[:, to * n_col:(to + 1) * n_col]
+        for r in range(1, n_aux):
+            c_copy(r).start()
+        g_ref[j] = 2.0 * coul[j] - c_send[j]
+        for r in range(1, n_aux):
+            c_copy(r).wait()
+            d = lax.rem(j + r, n_aux)
+            g_ref[d] = 2.0 * coul[d] - c_got[r - 1]
+
         for r in range(1, n_aux):
             my_copy(r).wait_send()
             for o in range(1, n_orb):
@@ -305,132 +381,44 @@
             for r in range(1, n_orb):
                 if u >= units - slots:
                     x_copy(u, r).wait_send()
-                x_copy(u, r).wait_recv()
 
     any_spec = pl.BlockSpec(memory_space=pl.ANY)
     vmem = pl.BlockSpec(memory_space=pltpu.VMEM)
     dma = pltpu.SemaphoreType.DMA
     return pl.pallas_call(
         kernel,
-        out_shape=(jax.ShapeDtypeStruct((n_orb, units, share, n_p), BF16), jax.ShapeDtypeStruct((units, share, n_p), F32),
-                   jax.ShapeDtypeStruct((n_d, n_m, n_col), F32)),
-        in_specs=[any_spec, vmem, vmem, vmem, any_spec],
-        out_specs=(any_spec, any_spec, vmem),
+        out_shape=(jax.ShapeDtypeStruct((n_d, n_m, n_col), F32), jax.ShapeDtypeStruct((n_orb, units, share, n_p), BF16),
+                   jax.ShapeDtypeStruct((units, share, n_p), F32)),
+        in_specs=[any_spec, vmem, vmem, vmem, any_spec, any_spec, any_spec],
+        out_specs=(vmem, any_spec, any_spec),
         scratch_shapes=[
             pltpu.VMEM((n_q, 2, sub, n_l), F32),
-            pltpu.VMEM((own_at + weights.shape[0], n_p), BF16),
+            pltpu.VMEM((own_at + len(order) * pad_q, n_p), BF16),
             pltpu.VMEM((n_v, LANES * sub, LANES), F32),
             pltpu.VMEM((2, n_d * n_i * sub, LANES), F32),
             pltpu.VMEM((n_t, LANES, n_di), F32),
             pltpu.VMEM((2, n_d, n_rows, pad_q), BF16),
             pltpu.VMEM((2, n_rows, 3 * pad_q), BF16),
             pltpu.VMEM((n_c, n_aux - 1, n_rows, pad_q), BF16),
-            pltpu.VMEM((n_orb, share, n_p), F32),
+            pltpu.VMEM((share, n_p), F32),
             pltpu.VMEM((slots, n_orb, share, n_p), BF16),
             pltpu.VMEM((n_g_rows, pad_q), F32), pltpu.VMEM((n_orb - 1, n_g_rows, pad_q), F32),
             pltpu.VMEM((n_g_rows, n_p), F32), pltpu.VMEM((n_aux - 1, n_g_rows, n_p), F32),
             pltpu.VMEM((n_g_rows, pad_q), F32), pltpu.SMEM((n_g_rows, pad_q), F32),
-            pltpu.VMEM((n_aux, n_d, n_m, n_col), F32), pltpu.VMEM((n_aux - 1, n_d, n_m, n_col), F32),
+            pltpu.VMEM((n_aux, n_d, n_m, n_col), F32), pltpu.VMEM((n_aux - 1, n_d, n_m, n_col), F32), pltpu.VMEM((n_d, n_m, n_col), F32),
             dma((n_c, n_aux - 1, 2 + n_t)), dma((n_c, n_aux - 1, 2 + n_t)), dma((units, n_orb - 1)), dma((units, n_orb - 1)),
             dma((n_orb - 1,)), dma((n_orb - 1,)), dma((n_aux - 1,)), dma((n_aux - 1,)),
             dma((n_aux - 1,)), dma((n_aux - 1,)), dma((n_aux - 1, n_orb - 1)), dma((n_aux - 1, n_orb - 1)),
             dma((n_aux - 1,)), dma((n_aux - 1,)),
             dma((3,)), dma((2,)),
+            dma((2, 2 * n_c)), dma((len(order),)), dma((n_orb - 1,)), dma((n_orb - 1,)), dma((n_aux - 1,)), dma((n_aux - 1,)),
+            pltpu.VMEM((2, n_orb, n_c, group, n_p), BF16), pltpu.VMEM((2, n_c, group, n_p), F32),
+            pltpu.VMEM((n_l + 2 * n_m, n_l), F32), pltpu.VMEM((n_m, n_m), F32), pltpu.VMEM((n_l, n_l), F32),
+            pltpu.VMEM((n_orb, n_m, n_l), F32), pltpu.VMEM((n_orb - 1, n_m, n_l), F32),
+            pltpu.VMEM((n_aux, n_m, n_col), F32), pltpu.VMEM((n_aux - 1, n_m, n_col), F32),
         ],
         compiler_params=pltpu.CompilerParams(collective_id=0, has_side_effects=True, vmem_limit_bytes=67043328),
-    )(ints, c_cat, c_rows, pick, weights)
-
-
-def gram(t, mine, coul, n_aux):
-    n_k, n_c, n_i, n_r, n_p = t.shape
-    n_m, n_n = n_c * n_r, n_k * n_c * n_r
-    n_col = n_n // n_aux
-
-    def kernel(t_hbm, mine_hbm, coul_ref, g_ref, t_ref, mine_ref, acc, sq, side, k_send, k_got, c_send, c_got,
-               load, load_m, ks_send, ks_recv, cs_send, cs_recv):
-        j, k = lax.axis_index('aux'), lax.axis_index('orb')
-
-        def load_t(i):
-            return pltpu.make_async_copy(t_hbm.at[:, :, i], t_ref.at[i], load.at[i])
-
-        def load_own(i):
-            return pltpu.make_async_copy(mine_hbm.at[:, i], mine_ref.at[i], load_m.at[i])
-
-        def k_copy(r):
-            to = lax.rem(k + r, n_k)
-            return pltpu.make_async_remote_copy(
-                src_ref=k_send.at[to], dst_ref=k_got.at[r - 1], send_sem=ks_send.at[r - 1], recv_sem=ks_recv.at[r - 1],
-                device_id={'orb': to}, device_id_type=MESH)
-
-        def c_copy(r):
-            to = lax.rem(j + n_aux - r, n_aux)
-            return pltpu.make_async_remote_copy(
-                src_ref=c_send.at[to], dst_ref=c_got.at[r - 1], send_sem=cs_send.at[r - 1], recv_sem=cs_recv.at[r - 1],
-                device_id={'aux': to}, device_id_type=MESH)
-
-        for i in range(n_i):
-            load_t(i).start()
-            load_own(i).start()
-        barrier = pltpu.get_barrier_semaphore()
-        for r in range(1, n_aux):
-            pl.semaphore_signal(barrier, inc=1, device_id={'aux': lax.rem(j + r, n_aux)}, device_id_type=MESH)
-        for r in range(1, n_k):
-            pl.semaphore_signal(barrier, inc=1, device_id={'orb': lax.rem(k + r, n_k)}, device_id_type=MESH)
-        acc[...] = jnp.zeros_like(acc)
-        sq[...] = jnp.zeros_like(sq)
-        nt = (((1,), (1,)), ((), ()))
-
-        @pl.loop(0, n_i)
-        def _(i):
-            load_t(i).wait()
-            load_own(i).wait()
-            all_t = t_ref[i].reshape(n_n, n_p)
-            own = mine_ref[i].reshape(n_m, n_p)
-            _, mid, low = parts3(own)
-            left = jnp.concatenate([all_t, mid, low], axis=0)
-            acc[...] += lax.dot_general(left, all_t, nt, preferred_element_type=F32)
-            sq[...] += lax.dot_general(mid, mid, nt, preferred_element_type=F32)
-
-        put = lax.broadcasted_iota(jnp.int32, (n_m, n_n), 1) == lax.broadcasted_iota(jnp.int32, (n_m, n_n), 0) + k * n_m
-        own_sq = jnp.dot(0.5 * sq[...], put.astype(F32), precision=PRECISE, preferred_element_type=F32)
-        side[...] = jnp.zeros_like(side)
-        side[pl.ds(pl.multiple_of(k * n_m, 8), n_m), :] = acc[n_n:n_n + n_m, :] + acc[n_n + n_m:, :] + own_sq
-        k_send[...] = (acc[:n_n, :] + side[...] + side[...].T).reshape(n_k, n_m, n_n)
-        pl.semaphore_wait(barrier, n_aux + n_k - 2)
-        for r in range(1, n_k):
-            k_copy(r).start()
-        for r in range(1, n_k):
-            k_copy(r).wait()
-        total = k_send[k]
-        for r in range(1, n_k):
-            total += k_got[r - 1]
-        for to in range(n_aux):
-            c_send[to] = total[:, to * n_col:(to + 1) * n_col]
-        for r in range(1, n_aux):
-            c_copy(r).start()
-        g_ref[j] = 2.0 * coul_ref[j] - c_send[j]
-        for r in range(1, n_aux):
-            c_copy(r).wait()
-            d = lax.rem(j + r, n_aux)
-            g_ref[d] = 2.0 * coul_ref[d] - c_got[r - 1]
-
-    any_spec = pl.BlockSpec(memory_space=pl.ANY)
-    vmem = pl.BlockSpec(memory_space=pltpu.VMEM)
-    dma = pltpu.SemaphoreType.DMA
-    return pl.pallas_call(
-        kernel,
-        out_shape=jax.ShapeDtypeStruct((n_aux, n_m, n_col), F32),
-        in_specs=[any_spec, any_spec, vmem],
-        out_specs=vmem,
-        scratch_shapes=[
-            pltpu.VMEM((n_i, n_k, n_c, n_r, n_p), BF16), pltpu.VMEM((n_i, n_c, n_r, n_p), F32),
-            pltpu.VMEM((n_n + 2 * n_m, n_n), F32), pltpu.VMEM((n_m, n_m), F32), pltpu.VMEM((n_n, n_n), F32),
-            pltpu.VMEM((n_k, n_m, n_n), F32), pltpu.VMEM((n_k - 1, n_m, n_n), F32),
-            pltpu.VMEM((n_aux, n_m, n_col), F32), pltpu.VMEM((n_aux - 1, n_m, n_col), F32),
-            dma((n_i,)), dma((n_i,)), dma((n_k - 1,)), dma((n_k - 1,)), dma((n_aux - 1,)), dma((n_aux - 1,)),
-        ],
-        compiler_params=pltpu.CompilerParams(collective_id=1, has_side_effects=True, vmem_limit_bytes=67043328),
-    )(t, mine, coul)
+    )(ints, c_cat, c_rows, pick, *parts)[0]
 
 
 def solution(mesh):
@@ -440,7 +428,6 @@
         n_q, n_m, n_l = ints.shape
         n_d, _, n_i = orbitals.shape
         n_p = n_aux * n_q
-        n_c = n_m // (2 * SUB)
         pad_p = round_up(n_p, LANES)
         n_t = n_q // Q_TILE
         pad_q = n_t * LANES
@@ -448,18 +435,13 @@
         k = lax.axis_index('orb')
 
         metric_pad = jnp.pad(metric.reshape(n_t, Q_TILE, n_p), ((0, 0), (0, LANES - Q_TILE), (0, pad_p - n_p))).reshape(pad_q, pad_p)
-        m_hi, m_mid, m_low = split3(metric_pad)
-        fit_w = jnp.concatenate([m_hi, m_mid, m_low, m_hi, m_mid, m_hi], axis=0)
-
         c_all = jnp.pad(orbitals.transpose(1, 0, 2).reshape(n_l, n_d * n_i), ((0, 0), (0, pad_di - n_d * n_i)))
         c_hi, c_mid, c_low = split3(c_all)
         c_cat = jnp.concatenate([c_hi, c_mid, c_low, c_hi, c_mid, c_hi], axis=0)
         c_rows = lax.dynamic_slice_in_dim(c_all, k * n_m, n_m, axis=0)
         lane = jnp.arange(pad_di)[None, :] // n_i
         pick = (lane == jnp.arange(2 * SUB)[:, None]).astype(F32)
-        all_t, mine, coul = fit_exchange(ints.reshape(n_q, n_m // SUB, SUB, n_l), c_cat, c_rows.reshape(n_m // SUB, SUB, pad_di), pick, fit_w, n_aux, n_orb, n_i)
-        all_t = all_t.reshape(n_orb, n_c, n_i // n_orb, 2 * SUB, pad_p)
-        mine = mine.reshape(n_c, n_i // n_orb, 2 * SUB, pad_p)
-        return gram(all_t, mine, coul, n_aux)
+        return fock(ints.reshape(n_q, n_m // SUB, SUB, n_l), c_cat, c_rows.reshape(n_m // SUB, SUB, pad_di), pick, split3(metric_pad),
+                    n_aux, n_orb, n_i)
 
     return jax.shard_map(local_fock, mesh=mesh, in_specs=(P(('sys', 'aux'), 'orb', None), P(('sys', 'aux'), None), P('sys', None, None)), out_specs=P('sys', 'orb', 'aux'), check_vma=False)

time: 248 us -> 237 us (0.956)
  Pallas kernels: 232 us -> 225 us
  local copies, waits for them, and re-layouts: 10.1 us -> 3.59 us
    pallas_call x2 -> x1, Pallas kernels: 232 us -> 225 us  [fock(): pl.pallas_call(kernel, out_shape=(jax.ShapeDtypeStruct((n_d, n_m, n_col),...]
    unnamed x8 -> x3, local copies, waits for them, and re-layouts: 6.99 us -> 1.54 us
where the time goes in v3:
time: 237 us; the launch traced here: 236 us
  Pallas kernels  225 us (95%)
  other arithmetic  7.45 us (3%)
  local copies, waits for them, and re-layouts  3.59 us (2%)
    pallas_call x1, Pallas kernels, fock(): pl.pallas_call(kernel, out_shape=(jax.ShapeDtypeStruct((n_d, n_m, n_col),...  225 us

profile of v3, /device:TPU:97, one launch (start us, length us, event | category | flops | bytes accessed | tf_op | source)
XLA Modules:
  0.0 236.4 jit_solution(15683825737574241083)
XLA Ops:
  0.0 0.6 fusion.4.pick_ref
  0.6 1.3 copy.5
  1.9 0.6 fusion.3.crow_ref
  2.5 0.8 constant_dynamic-update-slice_fusion.4
  3.3 0.8 constant_dynamic-update-slice_fusion.3
  4.0 0.0 copy-start
  4.0 0.8 fusion.2
  4.9 0.7 constant_dynamic-update-slice_fusion.2
  5.6 0.8 constant_dynamic-update-slice_fusion.1
  6.4 0.7 constant_dynamic-update-slice_fusion.c_ref
  7.2 0.0 copy-done
  7.2 0.1 pad.9
  7.3 2.2 fusion
  9.5 225.3 %shard_map.37 = (f32[4,48,96]{2,1,0:T(8,128)}, bf16[8,6,80,1408]{3,2,1,0:T(8,128)(2,1)}, f32[6,80,1408]{2,1,0:T(8,128)}) custom-call(f32[336,6,8,384]{3,2,1,0:T(8,128)} %bitcast.14, bf16[2304,384]{1,0:T(8,128)(2,1)} %constant_dynamic-update-slice_fusion.c_ref, f32[6,8,384]{2,1,0:T(8,128)} %fusion.3.crow_ref, f32[16,384]{1,0:T(8,128)} %fusion.4.pick_ref, ...), custom_call_target="tpu_custom_call" | custom-call | tf_op jit(solution)/shard_map/pallas_call | solution.py:388
  234.8 1.5 copy.12
  (1 shorter events, 0.0 us)
Async XLA Ops:
  4.0 3.1 %copy-start = (f32[336,1344]{1,0:T(8,128)S(1)}, f32[336,1344]{1,0:T(8,128)}, u32[]{:S(2)}) copy-start(f32[336,1344]{1,0:T(8,128)} %param.4) | copy-start | bytes 5419012

commit v4 on v3

--- a/solution.py
+++ b/solution.py
@@ -273,8 +273,8 @@
         to_smem.start()
         to_smem.wait()
         for c in range(n_c):
-            if c > 0:
-                fit_half(2, c - 1)
+            if c < 2:
+                fit_half(2, c)
             load_b(c).wait()
             for h in range(2):
                 total = [jnp.zeros((sub, n_l), F32) for _ in range(n_d)]

time: 237 us -> 233 us (0.983)
  Pallas kernels: 225 us -> 222 us
    pallas_call x1, Pallas kernels: 225 us -> 222 us  [fock(): pl.pallas_call(kernel, out_shape=(jax.ShapeDtypeStruct((n_d, n_m, n_col),...]
where the time goes in v4:
time: 233 us
  Pallas kernels  222 us (95%)
  other arithmetic  7.45 us (3%)
  local copies, waits for them, and re-layouts  3.59 us (2%)
    pallas_call x1, Pallas kernels, fock(): pl.pallas_call(kernel, out_shape=(jax.ShapeDtypeStruct((n_d, n_m, n_col),...  222 us

profile of v4, /device:TPU:97, one launch (start us, length us, event | category | flops | bytes accessed | tf_op | source)
XLA Modules:
  0.0 232.8 jit_solution(12604208052320850154)
XLA Ops:
  0.0 0.6 fusion.4.pick_ref
  0.6 1.3 copy.5
  1.9 0.6 fusion.3.crow_ref
  2.5 0.8 constant_dynamic-update-slice_fusion.4
  3.3 0.8 constant_dynamic-update-slice_fusion.3
  4.0 0.0 copy-start
  4.0 0.8 fusion.2
  4.9 0.7 constant_dynamic-update-slice_fusion.2
  5.6 0.8 constant_dynamic-update-slice_fusion.1
  6.4 0.7 constant_dynamic-update-slice_fusion.c_ref
  7.2 0.0 copy-done
  7.2 0.1 pad.9
  7.3 2.2 fusion
  9.5 221.8 %shard_map.37 = (f32[4,48,96]{2,1,0:T(8,128)}, bf16[8,6,80,1408]{3,2,1,0:T(8,128)(2,1)}, f32[6,80,1408]{2,1,0:T(8,128)}) custom-call(f32[336,6,8,384]{3,2,1,0:T(8,128)} %bitcast.14, bf16[2304,384]{1,0:T(8,128)(2,1)} %constant_dynamic-update-slice_fusion.c_ref, f32[6,8,384]{2,1,0:T(8,128)} %fusion.3.crow_ref, f32[16,384]{1,0:T(8,128)} %fusion.4.pick_ref, ...), custom_call_target="tpu_custom_call" | custom-call | tf_op jit(solution)/shard_map/pallas_call | solution.py:388
  231.3 1.5 copy.12
  (1 shorter events, 0.0 us)
Async XLA Ops:
  4.0 3.1 %copy-start = (f32[336,1344]{1,0:T(8,128)S(1)}, f32[336,1344]{1,0:T(8,128)}, u32[]{:S(2)}) copy-start(f32[336,1344]{1,0:T(8,128)} %param.4) | copy-start | bytes 5419012
